TPU v7x, 8 devices: a whole 2x2x1 slice. The times are simulated.
8 devices in a mesh: dp: 1 (over z), tp: 8 (over y, x, core).
Axes of the slice: x: 2, y: 2, z: 1, core: 2. Of those that a mesh axis runs over, the one named last changes fastest.
Arguments:
- tok_hidden: bfloat16 [256, 2048], P('dp')
- seq_lens: int32 [256], P('dp')
- k_cache: bfloat16 [256, 512, 8, 64], P('dp', None, 'tp')
- v_cache: bfloat16 [256, 512, 8, 64], P('dp', None, 'tp')
- next_tok: int32 [256], P('dp')
- g_attn: bfloat16 [2048], replicated
- w_q: bfloat16 [2048, 2048], P(None, 'tp')
- b_q: bfloat16 [2048], P('tp')
- w_k: bfloat16 [2048, 512], P(None, 'tp')
- b_k: bfloat16 [512], P('tp')
- w_v: bfloat16 [2048, 512], P(None, 'tp')
- b_v: bfloat16 [512], P('tp')
- w_o: bfloat16 [2048, 2048], P('tp')
- g_mlp: bfloat16 [2048], replicated
- w_gate: bfloat16 [2048, 8192], P(None, 'tp')
- w_up: bfloat16 [2048, 8192], P(None, 'tp')
- w_down: bfloat16 [8192, 2048], P('tp')
- g_final: bfloat16 [2048], replicated
- w_head: bfloat16 [128256, 2048], P('tp')
Outputs:
- output 1: bfloat16 [256, 2048], P('dp')
- output 2: bfloat16 [256, 512, 8, 64], P('dp', None, 'tp')
- output 3: bfloat16 [256, 512, 8, 64], P('dp', None, 'tp')
- output 4: float32 [256], P('dp')
- output 5: float32 [256], P('dp')
All inputs are finite; a program needn't handle non-finite values.
Results may differ from a plain program's by a relative error of at most 0.0134547.
Values are sent between devices in bfloat16 or wider.
A program may use at most 1 GiB of HBM per device.

v0:
```python
import jax
import jax.numpy as jnp
from jax import lax
from jax.sharding import PartitionSpec as P

THETA = 1000000.0
EPS = 1e-6


def rms_norm(values, gain_vec):
    vals_f32 = values.astype(jnp.float32)
    inv_rms = lax.rsqrt(jnp.mean(vals_f32 * vals_f32, axis=-1, keepdims=True) + EPS)
    return (vals_f32 * inv_rms * gain_vec.astype(jnp.float32)).astype(jnp.bfloat16)


def rotary(values, positions):
    half_dim = values.shape[-1] // 2
    inv_freq = jnp.power(THETA, jnp.arange(half_dim, dtype=jnp.float32) * (-2.0 / values.shape[-1]))
    angles = positions.astype(jnp.float32)[:, None] * inv_freq[None, :]
    cos_part = jnp.cos(angles)[:, None, :]
    sin_part = jnp.sin(angles)[:, None, :]
    first_half = values[..., :half_dim]
    second_half = values[..., half_dim:]
    return jnp.concatenate([first_half * cos_part - second_half * sin_part, second_half * cos_part + first_half * sin_part], axis=-1)


def attention_block(tok_hidden, seq_lens, k_cache, v_cache, g_attn, w_q, b_q, w_k, b_k, w_v, b_v):
    num_rows = tok_hidden.shape[0]
    cache_len = k_cache.shape[1]
    slot_count = k_cache.shape[2]
    head_dim = k_cache.shape[3]
    head_count = w_q.shape[1] // head_dim
    group_size = head_count // slot_count
    normed = rms_norm(tok_hidden, g_attn)
    q_proj = jnp.dot(normed, w_q, preferred_element_type=jnp.float32) + b_q.astype(jnp.float32)
    k_proj = jnp.dot(normed, w_k, preferred_element_type=jnp.float32) + b_k.astype(jnp.float32)
    v_proj = jnp.dot(normed, w_v, preferred_element_type=jnp.float32) + b_v.astype(jnp.float32)
    q_rot = rotary(q_proj.reshape(num_rows, head_count, head_dim), seq_lens).astype(jnp.bfloat16)
    k_new = rotary(k_proj.reshape(num_rows, slot_count, head_dim), seq_lens).astype(jnp.bfloat16)
    v_new = v_proj.reshape(num_rows, slot_count, head_dim).astype(jnp.bfloat16)
    slot_ids = lax.broadcasted_iota(jnp.int32, (1, cache_len, 1, 1), 1)
    write_mask = slot_ids == seq_lens[:, None, None, None]
    k_all = jnp.where(write_mask, k_new[:, None], k_cache)
    v_all = jnp.where(write_mask, v_new[:, None], v_cache)
    q_grp = q_rot.reshape(num_rows, slot_count, group_size, head_dim)
    scores = jnp.einsum('bkgd,blkd->bkgl', q_grp, k_all, preferred_element_type=jnp.float32) * (head_dim ** -0.5)
    score_ids = lax.broadcasted_iota(jnp.int32, (1, 1, 1, cache_len), 3)
    scores = jnp.where(score_ids <= seq_lens[:, None, None, None], scores, -jnp.inf)
    row_max = jnp.max(scores, axis=-1, keepdims=True)
    exp_scores = jnp.exp(scores - row_max)
    attn_probs = (exp_scores / jnp.sum(exp_scores, axis=-1, keepdims=True)).astype(jnp.bfloat16)
    attn_vals = jnp.einsum('bkgl,blkd->bkgd', attn_probs, v_all, preferred_element_type=jnp.float32)
    attn_out = attn_vals.astype(jnp.bfloat16).reshape(num_rows, head_count * head_dim)
    return attn_out, k_all, v_all


def local_step(tok_hidden, seq_lens, k_cache, v_cache, next_tok, g_attn, w_q, b_q, w_k, b_k, w_v, b_v, w_o, g_mlp, w_gate, w_up, w_down, g_final, w_head):
    attn_out, k_all, v_all = attention_block(tok_hidden, seq_lens, k_cache, v_cache, g_attn, w_q, b_q, w_k, b_k, w_v, b_v)
    attn_part = jnp.dot(attn_out, w_o, preferred_element_type=jnp.float32).astype(jnp.bfloat16)
    attn_sum = lax.psum(attn_part, 'tp')
    residual = (tok_hidden.astype(jnp.float32) + attn_sum.astype(jnp.float32)).astype(jnp.bfloat16)
    mlp_in = rms_norm(residual, g_mlp)
    gate_proj = jnp.dot(mlp_in, w_gate, preferred_element_type=jnp.float32)
    up_proj = jnp.dot(mlp_in, w_up, preferred_element_type=jnp.float32)
    hidden = (jax.nn.silu(gate_proj) * up_proj).astype(jnp.bfloat16)
    down_part = jnp.dot(hidden, w_down, preferred_element_type=jnp.float32).astype(jnp.bfloat16)
    down_sum = lax.psum(down_part, 'tp')
    y_out = (residual.astype(jnp.float32) + down_sum.astype(jnp.float32)).astype(jnp.bfloat16)
    final_norm = rms_norm(y_out, g_final)
    logits = lax.dot_general(final_norm, w_head, (((1,), (1,)), ((), ())), preferred_element_type=jnp.float32)
    vocab_loc = w_head.shape[0]
    vocab_ids = lax.broadcasted_iota(jnp.int32, (1, vocab_loc), 1)
    local_tok = next_tok - lax.axis_index('tp') * vocab_loc
    local_max = jnp.max(logits, axis=1)
    local_sum = jnp.sum(jnp.exp(logits - local_max[:, None]), axis=1)
    local_target = jnp.sum(jnp.where(vocab_ids == local_tok[:, None], logits, 0.0), axis=1)
    all_stats = lax.all_gather(jnp.stack([local_max, local_sum, local_target]), 'tp')
    glob_max = jnp.max(all_stats[:, 0], axis=0)
    exp_total = jnp.sum(all_stats[:, 1] * jnp.exp(all_stats[:, 0] - glob_max[None, :]), axis=0)
    norm_lse = glob_max + jnp.log(exp_total)
    tok_logp = jnp.sum(all_stats[:, 2], axis=0) - norm_lse
    return y_out, k_all, v_all, tok_logp, norm_lse


def solution(mesh):
    row_spec = P('dp', None)
    vec_spec = P('dp')
    cache_spec = P('dp', None, 'tp', None)
    col_spec = P(None, 'tp')
    part_spec = P('tp')
    whole_spec = P(None)
    in_specs = (row_spec, vec_spec, cache_spec, cache_spec, vec_spec, whole_spec, col_spec, part_spec, col_spec, part_spec, col_spec, part_spec, P('tp', None), whole_spec, col_spec, col_spec, P('tp', None), whole_spec, P('tp', None))
    out_specs = (row_spec, cache_spec, cache_spec, vec_spec, vec_spec)
    return jax.shard_map(local_step, mesh=mesh, in_specs=in_specs, out_specs=out_specs, check_vma=False)
```

profile of v0, /device:TPU:0, one launch (start us, length us, event | category | flops | bytes accessed | tf_op | source)
XLA Modules:
  0.0 234.1 jit_solution(5107749694317428525)
XLA Ops:
  7.2 0.0 copy-start
  7.2 0.0 copy-start.2
  7.2 0.0 copy-start.9
  7.2 0.0 copy-start.8
  7.2 0.0 all-reduce.3.cloned.1.call-start
  7.3 0.8 convert_element_type.89
  8.1 1.5 iota_compare_fusion.2
  9.6 0.7 convert_element_type.86
  10.3 1.5 fusion.8
  11.8 0.7 convert_element_type.90
  12.5 1.2 multiply_cosine_fusion
  13.7 1.8 fusion.21
  15.5 0.2 fusion.48
  15.7 0.7 copy.37
  16.5 0.0 copy-done.9
  16.5 0.0 copy-done.2
  16.5 0.0 copy-done.8
  16.5 0.5 fusion.22
  17.0 0.7 copy.38
  17.7 0.0 copy-done.10
  17.7 1.9 convolution_add_fusion
  19.6 0.2 copy.42
  19.9 0.2 copy.43
  20.1 1.9 subtract_convert_fusion
  22.1 24.0 %broadcast_select_fusion.1 = (bf16[256,512,1,64]{1,3,2,0:T(8,128)(2,1)}, bf16[256,512,1,64]{1,3,2,0:T(8,128)(2,1)}) fusion(bf16[256,512,1,64]{1,3,2,0:T(8,128)(2,1)} %param.21, pred[256,512]{1,0:T(8,128)(4,1)} %get-tuple-element.28, bf16[256,64]{1,0:T(8,128)(2,1)} %copy.37, bf16[256,512,1,64]{1,3,2,0:T(8,128)(2,1)} %param.22, bf16[256,64]{1,0:T(8,128)(2,1)} %copy.38), kind=kLoop, calls=%fused_computation.6 | loop fusion | flops 16777216 | bytes 67305472 | tf_op jit(solution)/shard_map/jit(_where)/select_n | solution.py:43
  46.0 0.0 copy-done.3
  46.0 8.3 %fusion.63 = (f32[256,4]{1,0:T(8,128)S(1)}, f32[256,4,512]{2,1,0:T(4,128)}) fusion(pred[256,512]{1,0:T(8,128)(4,1)S(1)} %get-tuple-element.27, bf16[256,512,1,64]{1,3,2,0:T(8,128)(2,1)} %get-tuple-element.19, bf16[256,4,32]{2,1,0:T(4,128)(2,1)S(1)} %copy-done.3, bf16[256,4,32]{2,1,0:T(4,128)(2,1)S(1)} %get-tuple-element.15), kind=kOutput, calls=%fused_computation.94 | convolution fusion | flops 69468672 | bytes 19140608 | tf_op jit(solution)/shard_map/sub | solution.py:50
  54.3 10.9 %fusion.18 = bf16[256,4,64]{2,1,0:T(4,128)(2,1)S(1)} fusion(bf16[256,512,1,64]{1,3,2,0:T(8,128)(2,1)} %get-tuple-element.20, f32[256,4,512]{2,1,0:T(4,128)} %get-tuple-element.30, f32[256,4]{1,0:T(8,128)S(1)} %get-tuple-element.29), kind=kOutput, calls=%fused_computation.37 | convolution fusion | flops 68222976 | bytes 19009536 | tf_op jit(solution)/shard_map/bkgl,blkd->bkgd/dot_general | solution.py:52
  65.2 0.2 copy.39
  65.4 0.0 copy-done
  65.4 1.4 convolution_convert_fusion.1
  66.8 0.0 all-reduce.3.cloned.1.call-update
  66.9 0.2 all-reduce.5.cloned.1.call-start
  67.1 0.0 copy-done.5
  67.1 48.0 %all-reduce.3.cloned.1.call-done = bf16[256,2048]{1,0:T(8,128)(2,1)} async-done(((bf16[256,2048]{1,0:T(8,128)(2,1)}), bf16[256,2048]{1,0:T(8,128)(2,1)}) %all-reduce.3.cloned.1.call-update) | async-done | bytes 1048592 | tf_op jit(solution)/shard_map/psum | solution.py:60
  115.1 1.7 fusion.12
  116.8 3.5 %fusion.34 = f32[256,1024]{1,0:T(8,128)S(1)} fusion(bf16[2048,1024]{1,0:T(8,128)(2,1)} %param.33, bf16[256,2048]{1,0:T(8,128)(2,1)S(1)} %get-tuple-element.14, f32[2048]{0:T(1024)S(1)} %convert_element_type.99, f32[256]{0:T(256)S(1)} %add_rsqrt_fusion.1), kind=kOutput, calls=%fused_computation.55 | convolution fusion | flops 1075838976 | bytes 6300672 | tf_op jit(solution)/shard_map/dot_general | solution.py:63
  120.3 0.0 copy-start.6
  120.3 0.0 copy-start.7
  120.3 7.0 %convolution_convert_fusion = bf16[256,2048]{1,0:T(8,128)(2,1)} fusion(bf16[1024,2048]{1,0:T(8,128)(2,1)} %param.35, bf16[2048,1024]{1,0:T(8,128)(2,1)} %param.34, f32[256,1024]{1,0:T(8,128)S(1)} %fusion.34, bf16[256,2048]{1,0:T(8,128)(2,1)S(1)} %get-tuple-element.14, f32[2048]{0:T(1024)S(1)} %convert_element_type.99, f32[256]{0:T(256)S(1)} %add_rsqrt_fusion.1), kind=kOutput, calls=%fused_computation.18 | convolution fusion | flops 2151677952 | bytes 11543552 | tf_op jit(solution)/shard_map/dot_general | solution.py:66
  127.4 0.0 all-reduce.5.cloned.1.call-update
  127.4 44.6 %all-reduce.5.cloned.1.call-done = bf16[256,2048]{1,0:T(8,128)(2,1)} async-done(((bf16[256,2048]{1,0:T(8,128)(2,1)}), bf16[256,2048]{1,0:T(8,128)(2,1)}) %all-reduce.5.cloned.1.call-update) | async-done | bytes 1048592 | tf_op jit(solution)/shard_map/psum | solution.py:67
  172.1 1.7 fusion.5
  173.8 0.0 copy-start.4
  173.8 33.8 %fusion.64 = (f32[256]{0:T(256)S(1)}, f32[256,16032]{0,1:T(8,128)}) fusion(bf16[16032,2048]{1,0:T(8,128)(2,1)} %param.37, bf16[256,2048]{1,0:T(8,128)(2,1)S(1)} %get-tuple-element.12, f32[2048]{0:T(1024)S(1)} %convert_element_type.106, f32[256]{0:T(256)S(1)} %add_rsqrt_fusion), kind=kOutput, calls=%fused_computation.95 | convolution fusion | flops 16816971776 | bytes 83142656 | tf_op jit(solution)/shard_map/dot_general | solution.py:70
  207.6 8.0 %exponential_reduce_fusion = (f32[256]{0:T(256)S(1)}, f32[256]{0:T(256)S(1)}) fusion(f32[256,16032]{0,1:T(8,128)} %get-tuple-element.32, f32[256]{0:T(256)S(1)} %get-tuple-element.31, s32[256]{0:T(256)S(1)} %broadcast_subtract_fusion), kind=kLoop, calls=%fused_computation.9 | loop fusion | flops 20520448 | bytes 16420864 | tf_op jit(solution)/shard_map/reduce_sum | solution.py:75
  215.7 11.0 %all-gather.1 = f32[8,3,256]{2,1,0:T(4,128)S(1)} all-gather(f32[1,3,256]{2,1,0:T(4,128)S(1)} %maximum_bitcast_fusion), channel_id=2, replica_groups=mesh['dp'=1,'tp'=8] {'tp'}, dimensions={0}, use_global_device_ids=true | all-gather | bytes 27648 | tf_op jit(solution)/shard_map/all_gather | solution.py:77
  226.7 0.6 fusion.59
  (22 shorter events, 0.2 us)
Async XLA Ops:
  7.2 58.2 %copy-start = (bf16[256,2048]{1,0:T(8,128)(2,1)S(1)}, bf16[256,2048]{1,0:T(8,128)(2,1)}, u32[]{:S(2)}) copy-start(bf16[256,2048]{1,0:T(8,128)(2,1)} %param.31) | copy-start | bytes 3145732
  7.2 9.3 %copy-start.2 = (bf16[256,2048]{1,0:T(8,128)(2,1)S(1)}, bf16[256,2048]{1,0:T(8,128)(2,1)}, u32[]{:S(2)}) copy-start(bf16[256,2048]{1,0:T(8,128)(2,1)} %param.19) | copy-start | bytes 3145732
  7.2 9.3 %copy-start.9 = (bf16[64]{0:T(256)(128)(2,1)S(1)}, bf16[64]{0:T(256)(128)(2,1)}, u32[]{:S(2)}) copy-start(bf16[64]{0:T(256)(128)(2,1)} %param.30) | copy-start | bytes 388
  7.2 9.3 %copy-start.8 = (bf16[2048,64]{0,1:T(8,128)(2,1)S(1)}, bf16[2048,64]{0,1:T(8,128)(2,1)}, u32[]{:S(2)}) copy-start(bf16[2048,64]{0,1:T(8,128)(2,1)} %param.29) | copy-start | bytes 786436
  7.2 107.9 %all-reduce.3.cloned.1.call-start = ((), (), s32[]{:S(2)}) async-start(), calls=%async_computation | async-start | bytes 2097152 | tf_op jit(solution)/shard_map/psum | solution.py:60
  13.7 4.0 %copy-start.10 = (bf16[256]{0:T(256)(128)(2,1)S(1)}, bf16[256]{0:T(256)(128)(2,1)}, u32[]{:S(2)}) copy-start(bf16[256]{0:T(256)(128)(2,1)} %param.26) | copy-start | bytes 1540
  22.1 24.0 %copy-start.3 = (bf16[256,4,32]{2,1,0:T(4,128)(2,1)S(1)}, bf16[256,4,32]{2,1,0:T(4,128)(2,1)}, u32[]{:S(2)}) copy-start(bf16[256,4,32]{2,1,0:T(4,128)(2,1)} %get-tuple-element.16) | copy-start | bytes 196612
  65.2 1.9 copy-start.5
  66.9 105.2 %all-reduce.5.cloned.1.call-start = ((), (), s32[]{:S(2)}) async-start(), calls=%async_computation.1 | async-start | bytes 2097152 | tf_op jit(solution)/shard_map/psum | solution.py:67
  120.3 7.1 %copy-start.6 = (bf16[2048]{0:T(1024)(128)(2,1)S(1)}, bf16[2048]{0:T(1024)(128)(2,1)}, u32[]{:S(2)}) copy-start(bf16[2048]{0:T(1024)(128)(2,1)} %param.36) | copy-start | bytes 12292
  120.3 7.1 %copy-start.7 = (s32[256]{0:T(256)S(1)}, s32[256]{0:T(256)}, u32[]{:S(2)}) copy-start(s32[256]{0:T(256)} %param.23) | copy-start | bytes 3076
  173.8 33.8 %copy-start.4 = (bf16[256,2048]{1,0:T(8,128)(2,1)}, bf16[256,2048]{1,0:T(8,128)(2,1)S(1)}, u32[]{:S(2)}) copy-start(bf16[256,2048]{1,0:T(8,128)(2,1)S(1)} %get-tuple-element.12) | copy-start | bytes 3145732
  207.6 19.7 %copy-start.1 = (bf16[256,2048]{1,0:T(8,128)(2,1)S(1)}, bf16[256,2048]{1,0:T(8,128)(2,1)}, u32[]{:S(2)}) copy-start(bf16[256,2048]{1,0:T(8,128)(2,1)} %param.31) | copy-start | bytes 3145732
Sparse Core Ops, SparseCore 0:
  67.0 48.0 all-reduce.2
  127.5 44.5 all-reduce.4
where the time goes:
time: 235 us; the launch traced here: 234 us
  waiting for transfers between devices  92.6 us (39%)
  matrix products  69.1 us (29%)
  other arithmetic  44.8 us (19%)
  between operations  14.3 us (6%)
  blocking collectives  11 us (5%)
    psum x1, waiting for transfers between devices, local_step(): attn_sum = lax.psum(attn_part, 'tp')  48 us
    psum x1, waiting for transfers between devices, local_step(): down_sum = lax.psum(down_part, 'tp')  44.6 us
    dot_general x1, matrix products, local_step(): lax.dot_general(final_norm, w_head, (((1,), (1,)), ((), ())), preferred_e...  33.8 us
    select_n x1, other arithmetic, attention_block(): k_all = jnp.where(write_mask, k_new[:, None], k_cache)  24 us
    all_gather x1, blocking collectives, local_step(): lax.all_gather(jnp.stack([local_max, local_sum, local_target]), 'tp')  11 us
    dot_general x1, matrix products, attention_block(): jnp.einsum('bkgl,blkd->bkgd', attn_probs, v_all, preferred_element_type=j...  10.9 us
    sub x1, matrix products, attention_block(): exp_scores = jnp.exp(scores - row_max)  8.29 us
    reduce_sum x1, other arithmetic, local_step(): local_sum = jnp.sum(jnp.exp(logits - local_max[:, None]), axis=1)  8.05 us
  transfers between devices with their start and end apart: 2, of which 2 were waited for; matrix products, arithmetic and copies ran while one was open for 0% of the time, Pallas kernels for 0%

commit v1 on v0

v1 whole, which is shorter than its diff:
```python
import functools
import math

import jax
import jax.numpy as jnp
from jax import lax
from jax.experimental import pallas as pl
from jax.experimental.pallas import tpu as pltpu
from jax.sharding import PartitionSpec as P

THETA = 1000000.0
EPS = 1e-6
BATCH = 256
LMAX = 512
D = 2048
HEAD = 64
FF = 1024
STEP = 16
NSTEP = BATCH // STEP
BLK = STEP * HEAD
NBUF = 8
AHEAD = 5
COL = D // 8
HALF = BATCH // 2
VOC = 16032
VCH = 1024
NFULL = VOC // VCH
VTAIL = VOC - NFULL * VCH
NRING = 9

f32 = jnp.float32
bf16 = jnp.bfloat16
NT = (((1,), (1,)), ((), ()))
MESH = pl.DeviceIdType.MESH


def iota(shape, dim):
    return lax.broadcasted_iota(jnp.int32, shape, dim)


def attn_kernel(len_s, x_hbm, len_hbm, k_hbm, v_hbm, g_hbm, wq_hbm, bq_hbm, wk_hbm, bk_hbm, wv_hbm, bv_hbm, wo_hbm,
                ko_hbm, vo_hbm, part_ref,
                x_v, len_v, g_v, wq_v, bq_v, wkv_v, bk_v, bv_v, wo_v, kbuf, vbuf, normed, knv, qdup, lenc, attn,
                in_sem, krd, vrd, kwr, vwr):
    def load(src, dst, n):
        copy = pltpu.make_async_copy(src, dst, in_sem.at[n])
        copy.start()
        return copy

    small = [
        load(x_hbm, x_v, 0),
        load(g_hbm, g_v, 1),
        load(len_hbm, len_v, 2),
        load(wk_hbm, wkv_v.at[pl.ds(0, HEAD)], 3),
        load(wv_hbm, wkv_v.at[pl.ds(HEAD, HEAD)], 4),
        load(bk_hbm, bk_v, 5),
        load(bv_hbm, bv_v, 6),
        load(wq_hbm, wq_v, 7),
        load(bq_hbm, bq_v, 8),
    ]

    def read(i, hbm, buf, sem):
        slot = lax.rem(i, NBUF)
        return pltpu.make_async_copy(hbm.at[pl.ds(i * BLK, BLK)], buf.at[slot], sem.at[slot])

    def write(i, hbm, buf, sem):
        slot = lax.rem(i, NBUF)
        return pltpu.make_async_copy(buf.at[slot], hbm.at[pl.ds(i * BLK, BLK)], sem.at[slot])

    for i in range(AHEAD):
        read(i, k_hbm, kbuf, krd).start()
        read(i, v_hbm, vbuf, vrd).start()
    wo_copy = load(wo_hbm, wo_v, 9)
    for copy in small:
        copy.wait()

    @pl.loop(0, BATCH // 32)
    def _(r):
        rows = pl.ds(r * 32, 32)
        xr = x_v[rows, :].astype(f32)
        inv = lax.rsqrt(jnp.mean(xr * xr, axis=-1, keepdims=True) + EPS)
        normed[rows, :] = (xr * inv * g_v[...].astype(f32)).astype(bf16)

    freq = jnp.exp(iota((HEAD // 2, BATCH), 0).astype(f32) * (-2.0 / HEAD * math.log(THETA)))
    angles = jnp.broadcast_to(len_v[...].astype(f32), (HEAD // 2, BATCH)) * freq
    cos_t = jnp.cos(angles)
    sin_t = jnp.sin(angles)
    cos_q = jnp.concatenate([cos_t] * 4, axis=0).T
    sin_q = jnp.concatenate([sin_t] * 4, axis=0).T
    lenc[...] = jnp.broadcast_to(len_v[...], (128, BATCH)).astype(f32).T

    bias = jnp.concatenate([bk_v[...].astype(f32), bv_v[...].astype(f32)], axis=1)
    bias = jnp.broadcast_to(bias, (128, 128)).T
    bias = jnp.concatenate([bias, bias], axis=1)
    kv = lax.dot_general(wkv_v[...], normed[...], NT, preferred_element_type=f32) + bias
    first, second = kv[:HEAD // 2], kv[HEAD // 2:HEAD]
    kv = jnp.concatenate([first * cos_t - second * sin_t, second * cos_t + first * sin_t, kv[HEAD:]], axis=0)
    kv = kv.astype(bf16).astype(f32)
    for i in range(NSTEP):
        part = kv[:, (i // 8) * 128:(i // 8) * 128 + 128]
        shift = (128 - STEP * (i % 8)) % 128
        knv[i] = pltpu.roll(part, shift, 1) if shift else part

    q = jnp.dot(normed[...], wq_v[...], preferred_element_type=f32) + bq_v[...].astype(f32)
    lane = iota((BATCH, 128), 1)
    low = lane < HEAD
    early = lax.rem(lane, HEAD) < HEAD // 2
    for j in range(2):
        qa = q[:, j * 128:j * 128 + 128]
        rot = jnp.where(early, -pltpu.roll(qa, 96, 1), pltpu.roll(qa, 32, 1))
        qa = qa * cos_q + rot * sin_q
        swap = pltpu.roll(qa, HEAD, 1)
        qdup[2 * j] = jnp.where(low, qa, swap).astype(bf16)
        qdup[2 * j + 1] = jnp.where(low, swap, qa).astype(bf16)

    @pl.loop(0, NSTEP)
    def _(i):
        slot = lax.rem(i, NBUF)
        nxt = i + AHEAD

        @pl.when(nxt < NSTEP)
        def _():
            @pl.when(nxt >= NBUF)
            def _():
                write(nxt - NBUF, ko_hbm, kbuf, kwr).wait()
                write(nxt - NBUF, vo_hbm, vbuf, vwr).wait()
            read(nxt, k_hbm, kbuf, krd).start()
            read(nxt, v_hbm, vbuf, vrd).start()

        read(i, k_hbm, kbuf, krd).wait()
        read(i, v_hbm, vbuf, vrd).wait()

        lane_l = iota((HEAD, LMAX), 1)
        fresh = knv[i]
        for s in range(STEP):
            here = lane_l == len_s[i * STEP + s]
            rows = pl.ds(s * HEAD, HEAD)
            kcol = jnp.broadcast_to(fresh[:HEAD, s:s + 1], (HEAD, LMAX)).astype(bf16)
            vcol = jnp.broadcast_to(fresh[HEAD:, s:s + 1], (HEAD, LMAX)).astype(bf16)
            kbuf[slot, rows, :] = jnp.where(here, kcol, kbuf[slot, rows, :])
            vbuf[slot, rows, :] = jnp.where(here, vcol, vbuf[slot, rows, :])
        write(i, ko_hbm, kbuf, kwr).start()
        write(i, vo_hbm, vbuf, vwr).start()

        seqs = pl.ds(pl.multiple_of(i * STEP, STEP), STEP)
        diag = iota((STEP, BLK), 1) // HEAD == iota((STEP, BLK), 0)
        lhs = jnp.concatenate(
            [jnp.where(diag, jnp.concatenate([qdup[h, seqs, :]] * 8, axis=1), jnp.zeros((), bf16)) for h in range(4)], axis=0)
        scores = jnp.dot(lhs, kbuf[slot], preferred_element_type=f32) * (HEAD ** -0.5)
        limit = jnp.concatenate([lenc[seqs, :]] * 4, axis=0)
        limit = jnp.concatenate([limit] * 4, axis=1)
        scores = jnp.where(iota((4 * STEP, LMAX), 1).astype(f32) <= limit, scores, -jnp.inf)
        top = jnp.max(scores, axis=-1, keepdims=True)
        expd = jnp.exp(scores - top)
        probs = (expd / jnp.sum(expd, axis=-1, keepdims=True)).astype(bf16)
        out = lax.dot_general(probs, vbuf[slot], NT, preferred_element_type=f32)
        row_s = lax.rem(iota((4 * STEP, 128), 0), STEP)
        lane_s = iota((4 * STEP, 128), 1) // HEAD
        acc = jnp.zeros((4 * STEP, 128), f32)
        for j in range(8):
            acc = acc + jnp.where(row_s == lane_s + 2 * j, out[:, j * 128:j * 128 + 128], 0.0)
        acc = acc + pltpu.roll(acc, HEAD, 1)
        low16 = iota((STEP, 128), 1) < HEAD
        attn[seqs, :] = jnp.concatenate(
            [jnp.where(low16, acc[2 * j * STEP:(2 * j + 1) * STEP], acc[(2 * j + 1) * STEP:(2 * j + 2) * STEP]) for j in range(2)],
            axis=1).astype(bf16)

    wo_copy.wait()
    for d in range(8):
        prod = jnp.dot(attn[...], wo_v[:, d * COL:(d + 1) * COL], preferred_element_type=f32)
        part_ref[d % 2, d // 2] = prod.astype(bf16)
    for i in range(NSTEP - NBUF, NSTEP):
        write(i, ko_hbm, kbuf, kwr).wait()
        write(i, vo_hbm, vbuf, vwr).wait()


def attn_call(lens, x, k, v, g, wq, bq, wk, bk, wv, bv, wo):
    anyspec = pl.BlockSpec(memory_space=pl.ANY)
    cache = jax.ShapeDtypeStruct((BATCH * HEAD, LMAX), bf16)
    return pl.pallas_call(
        attn_kernel,
        out_shape=(cache, cache, jax.ShapeDtypeStruct((2, 4, BATCH, COL), bf16)),
        in_specs=[pl.BlockSpec(memory_space=pltpu.SMEM)] + [anyspec] * 12,
        out_specs=(anyspec, anyspec, pl.BlockSpec(memory_space=pltpu.VMEM)),
        scratch_shapes=[
            pltpu.VMEM((BATCH, D), bf16), pltpu.VMEM((1, BATCH), jnp.int32), pltpu.VMEM((1, D), bf16),
            pltpu.VMEM((D, 4 * HEAD), bf16), pltpu.VMEM((1, 4 * HEAD), bf16), pltpu.VMEM((2 * HEAD, D), bf16),
            pltpu.VMEM((1, HEAD), bf16), pltpu.VMEM((1, HEAD), bf16), pltpu.VMEM((4 * HEAD, D), bf16),
            pltpu.VMEM((NBUF, BLK, LMAX), bf16), pltpu.VMEM((NBUF, BLK, LMAX), bf16),
            pltpu.VMEM((BATCH, D), bf16), pltpu.VMEM((NSTEP, 128, 128), f32), pltpu.VMEM((4, BATCH, 128), bf16),
            pltpu.VMEM((BATCH, 128), f32), pltpu.VMEM((BATCH, 4 * HEAD), bf16),
            pltpu.SemaphoreType.DMA((10,)), pltpu.SemaphoreType.DMA((NBUF,)), pltpu.SemaphoreType.DMA((NBUF,)),
            pltpu.SemaphoreType.DMA((NBUF,)), pltpu.SemaphoreType.DMA((NBUF,)),
        ],
        compiler_params=pltpu.CompilerParams(vmem_limit_bytes=56 * 2**20),
        cost_estimate=pl.CostEstimate(flops=10**10, bytes_accessed=70 * 2**20, transcendentals=10**6),
        name="attn",
    )(lens, x, lens.reshape(1, BATCH), k, v, g, wq, bq, wk, bk, wv, bv, wo)


def tail_kernel(part_ref, x_hbm, tok_ref, gm_ref, gf_ref, wg_hbm, wu_hbm, wd_hbm, wh_hbm,
                y_ref, logp_ref, lse_ref,
                xown, wg_v, wu_v, wd_v, ring, part2, rs1, s2s, s2r, own, afull, yfull, mbuf, hid, fbuf, zbuf, stats, allst,
                in_sem, ring_sem, send_sem, recv_sem, st_send, st_recv):
    me = lax.axis_index("tp")
    core = lax.rem(me, 2)
    chip = me // 2
    partner = me + 1 - 2 * core
    chip_x = chip + 1 - 2 * lax.rem(chip, 2)
    chip_y = chip + 2 - 4 * (chip // 2)
    chip_d = 3 - chip
    others = (chip_x, chip_y, chip_d)

    def load(src, dst, n):
        copy = pltpu.make_async_copy(src, dst, in_sem.at[n])
        copy.start()
        return copy

    cols = pl.ds(pl.multiple_of(me * COL, COL), COL)
    xown_copy = load(x_hbm.at[:, cols], xown, 0)
    wg_copy = load(wg_hbm, wg_v, 1)
    wu_copy = load(wu_hbm, wu_v, 2)
    wd_copy = load(wd_hbm, wd_v, 3)

    def chunk(i):
        slot = lax.rem(i, NRING)
        return pltpu.make_async_copy(wh_hbm.at[pl.ds(i * VCH, VCH)], ring.at[slot], ring_sem.at[slot])

    tail_slot = NFULL % NRING
    tail_copy = pltpu.make_async_copy(wh_hbm.at[pl.ds(NFULL * VCH, VTAIL)], ring.at[tail_slot, pl.ds(0, VTAIL)],
                                      ring_sem.at[tail_slot])
    for i in range(NRING):
        chunk(i).start()

    barrier = pltpu.get_barrier_semaphore()
    for k in range(1, 8):
        pl.semaphore_signal(barrier, inc=1, device_id={"tp": lax.rem(me + k, 8)}, device_id_type=MESH)
    pl.semaphore_wait(barrier, 7)

    def remote(src, dst, n, dev):
        return pltpu.make_async_remote_copy(src_ref=src, dst_ref=dst, send_sem=send_sem.at[n], recv_sem=recv_sem.at[n],
                                            device_id={"tp": dev}, device_id_type=MESH)

    class Reduce:
        def __init__(self, which, half, part, full):
            self.base = (which * 2 + half) * 11
            self.which, self.half, self.part, self.full = which, half, part, full
            self.rows = pl.ds(half * HALF, HALF)

        def s1(self):
            return remote(self.part.at[1 - core, :, self.rows, :], rs1.at[self.which, self.half], self.base, partner)

        def s2(self, k):
            return remote(s2s.at[self.which, self.half, k], s2r.at[self.which, self.half, k], self.base + 1 + k,
                          2 * others[k] + core)

        def s3(self, k):
            block = self.full.at[me, self.rows]
            return remote(block, block, self.base + 4 + k, 2 * others[k] + core)

        def s3own(self):
            block = self.full.at[me, self.rows]
            return remote(block, block, self.base + 7, partner)

        def s4(self, k):
            block = self.full.at[2 * others[k] + core, self.rows]
            return remote(block, block, self.base + 8 + k, partner)

        def scatter(self):
            self.s1().wait_recv()
            for k in (2, 0, 1):
                total = self.part[core, others[k], self.rows, :].astype(f32) + rs1[self.which, self.half, others[k]].astype(f32)
                s2s[self.which, self.half, k] = total.astype(bf16)
                self.s2(k).start()
            own[self.which, self.half] = (self.part[core, chip, self.rows, :].astype(f32)
                                          + rs1[self.which, self.half, chip].astype(f32))

        def gather(self, resid):
            for k in range(3):
                self.s2(k).wait_recv()
            total = resid + own[self.which, self.half]
            for k in range(3):
                total = total + s2r[self.which, self.half, k].astype(f32)
            self.full[me, self.rows, :] = total.astype(bf16)
            for k in (2, 0, 1):
                self.s3(k).start()
            self.s3own().start()

        def forward(self):
            for k in range(3):
                self.s3(k).wait_recv()
                self.s4(k).start()

        def finish(self):
            self.s3own().wait_recv()
            for k in range(3):
                self.s4(k).wait_recv()

        def drain(self):
            self.s1().wait_send()
            self.s3own().wait_send()
            for k in range(3):
                self.s2(k).wait_send()
                self.s3(k).wait_send()
                self.s4(k).wait_send()

    first = [Reduce(0, h, part_ref, afull) for h in range(2)]
    second = [Reduce(1, h, part2, yfull) for h in range(2)]

    def norm_rows(full, half, gain_ref, dst, copy_to=None):
        @pl.loop(0, HALF // 32)
        def _(r):
            rows = pl.ds(pl.multiple_of(half * HALF + r * 32, 32), 32)
            total = jnp.zeros((32, 1), f32)
            for d in range(8):
                block = full[d, rows, :]
                if copy_to is not None:
                    copy_to[rows, d * COL:(d + 1) * COL] = block
                block = block.astype(f32)
                total = total + jnp.sum(block * block, axis=-1, keepdims=True)
            inv = lax.rsqrt(total * (1.0 / D) + EPS)
            for d in range(8):
                gain = gain_ref[:, d * COL:(d + 1) * COL].astype(f32)
                dst[rows, d * COL:(d + 1) * COL] = (full[d, rows, :].astype(f32) * inv * gain).astype(bf16)

    def gate_up(half):
        rows = pl.ds(half * HALF, HALF)
        for n in range(4):
            cs = slice(n * 256, (n + 1) * 256)
            gate = jnp.dot(mbuf[rows, :], wg_v[:, cs], preferred_element_type=f32)
            up = jnp.dot(mbuf[rows, :], wu_v[:, cs], preferred_element_type=f32)
            hid[rows, cs] = (gate / (1.0 + jnp.exp(-gate)) * up).astype(bf16)

    def down(half):
        rows = pl.ds(half * HALF, HALF)
        for d in range(8):
            prod = jnp.dot(hid[rows, :], wd_v[:, d * COL:(d + 1) * COL], preferred_element_type=f32)
            part2[d % 2, d // 2, rows, :] = prod.astype(bf16)

    for h in range(2):
        first[h].s1().start()
    for h in range(2):
        first[h].scatter()
    xown_copy.wait()
    for h in range(2):
        first[h].gather(xown[h * HALF:(h + 1) * HALF, :].astype(f32))
    first[0].forward()
    first[0].finish()
    norm_rows(afull, 0, gm_ref, mbuf)
    wg_copy.wait()
    wu_copy.wait()
    gate_up(0)
    first[1].forward()
    wd_copy.wait()
    down(0)
    second[0].s1().start()
    first[1].finish()
    norm_rows(afull, 1, gm_ref, mbuf)
    second[0].scatter()
    gate_up(1)
    down(1)
    second[1].s1().start()
    second[1].scatter()
    for h in range(2):
        second[h].gather(afull[me, h * HALF:(h + 1) * HALF, :].astype(f32))
    for h in range(2):
        second[h].forward()
    for h in range(2):
        second[h].finish()
        norm_rows(yfull, h, gf_ref, fbuf, y_ref)

    tok = tok_ref[...] - me * VOC

    def score(slot, size, base, state):
        top, total, target = state
        z = lax.dot_general(ring[slot, pl.ds(0, size), :], fbuf[...], NT, preferred_element_type=f32)
        zbuf[pl.ds(0, size), :] = z
        z = zbuf[pl.ds(0, size), :]
        new_top = jnp.maximum(top, jnp.max(z, axis=0, keepdims=True))
        total = total * jnp.exp(top - new_top) + jnp.sum(jnp.exp(z - new_top), axis=0, keepdims=True)
        hit = iota((size, BATCH), 0) == tok - base
        target = target + jnp.sum(jnp.where(hit, z, 0.0), axis=0, keepdims=True)
        return new_top, total, target

    def head_step(i, state):
        chunk(i).wait()
        state = score(lax.rem(i, NRING), VCH, i * VCH, state)
        nxt = i + NRING

        @pl.when(nxt < NFULL)
        def _():
            chunk(nxt).start()

        @pl.when(nxt == NFULL)
        def _():
            tail_copy.start()
        return state

    zero = jnp.zeros((1, BATCH), f32)
    state = (jnp.full((1, BATCH), -jnp.inf, f32), zero, zero)
    state = lax.fori_loop(0, NFULL, head_step, state)
    tail_copy.wait()
    top, total, target = score(tail_slot, VTAIL, NFULL * VCH, state)

    stats[...] = jnp.concatenate([top, total, target, zero, zero, zero, zero, zero], axis=0)
    allst[me] = stats[...]

    def stat_copy(k):
        return pltpu.make_async_remote_copy(src_ref=stats, dst_ref=allst.at[me], send_sem=st_send.at[k - 1],
                                            recv_sem=st_recv.at[k - 1], device_id={"tp": lax.rem(me + k, 8)},
                                            device_id_type=MESH)

    for k in range(1, 8):
        stat_copy(k).start()
    for k in range(1, 8):
        stat_copy(k).wait_recv()
    top = allst[0, 0:1, :]
    for d in range(1, 8):
        top = jnp.maximum(top, allst[d, 0:1, :])
    total = zero
    target = zero
    for d in range(8):
        total = total + allst[d, 1:2, :] * jnp.exp(allst[d, 0:1, :] - top)
        target = target + allst[d, 2:3, :]
    lse = top + jnp.log(total)
    lse_ref[...] = lse
    logp_ref[...] = target - lse
    for h in range(2):
        first[h].drain()
        second[h].drain()
    for k in range(1, 8):
        stat_copy(k).wait_send()


def tail_call(part, x, tok, gm, gf, wg, wu, wd, wh):
    anyspec = pl.BlockSpec(memory_space=pl.ANY)
    vspec = pl.BlockSpec(memory_space=pltpu.VMEM)
    row = jax.ShapeDtypeStruct((1, BATCH), f32)
    blocks = (2, 2, 3, HALF, COL)
    return pl.pallas_call(
        tail_kernel,
        out_shape=(jax.ShapeDtypeStruct((BATCH, D), bf16), row, row),
        in_specs=[vspec, anyspec, vspec, vspec, vspec, anyspec, anyspec, anyspec, anyspec],
        out_specs=(vspec, vspec, vspec),
        scratch_shapes=[
            pltpu.VMEM((BATCH, COL), bf16), pltpu.VMEM((D, FF), bf16), pltpu.VMEM((D, FF), bf16), pltpu.VMEM((FF, D), bf16),
            pltpu.VMEM((NRING, VCH, D), bf16), pltpu.VMEM((2, 4, BATCH, COL), bf16), pltpu.VMEM((2, 2, 4, HALF, COL), bf16),
            pltpu.VMEM(blocks, bf16), pltpu.VMEM(blocks, bf16), pltpu.VMEM((2, 2, HALF, COL), f32),
            pltpu.VMEM((8, BATCH, COL), bf16), pltpu.VMEM((8, BATCH, COL), bf16), pltpu.VMEM((BATCH, D), bf16),
            pltpu.VMEM((BATCH, FF), bf16), pltpu.VMEM((BATCH, D), bf16), pltpu.VMEM((VCH, BATCH), f32),
            pltpu.VMEM((8, BATCH), f32), pltpu.VMEM((8, 8, BATCH), f32),
            pltpu.SemaphoreType.DMA((4,)), pltpu.SemaphoreType.DMA((NRING,)), pltpu.SemaphoreType.DMA((44,)),
            pltpu.SemaphoreType.DMA((44,)), pltpu.SemaphoreType.DMA((7,)), pltpu.SemaphoreType.DMA((7,)),
        ],
        compiler_params=pltpu.CompilerParams(collective_id=0, has_side_effects=True, vmem_limit_bytes=63 * 2**20),
        cost_estimate=pl.CostEstimate(flops=2 * 10**10, bytes_accessed=80 * 2**20, transcendentals=10**6),
        name="tail",
    )(part, x, tok, gm, gf, wg, wu, wd, wh)


def local_step(x, lens, k_cache, v_cache, tok, g_attn, w_q, b_q, w_k, b_k, w_v, b_v, w_o, g_mlp, w_gate, w_up, w_down, g_final, w_head):
    def flat(cache):
        return cache.transpose(0, 2, 3, 1).reshape(BATCH * HEAD, LMAX)

    def unflat(cache):
        return cache.reshape(BATCH, 1, HEAD, LMAX).transpose(0, 3, 1, 2)

    k_new, v_new, part = attn_call(lens, x, flat(k_cache), flat(v_cache), g_attn.reshape(1, D), w_q, b_q.reshape(1, -1),
                                   w_k.T, b_k.reshape(1, -1), w_v.T, b_v.reshape(1, -1), w_o)
    y, logp, lse = tail_call(part, x, tok.reshape(1, BATCH), g_mlp.reshape(1, D), g_final.reshape(1, D), w_gate, w_up, w_down, w_head)
    return y, unflat(k_new), unflat(v_new), logp.reshape(BATCH), lse.reshape(BATCH)


def solution(mesh):
    row_spec = P('dp', None)
    vec_spec = P('dp')
    cache_spec = P('dp', None, 'tp', None)
    col_spec = P(None, 'tp')
    part_spec = P('tp')
    whole_spec = P(None)
    in_specs = (row_spec, vec_spec, cache_spec, cache_spec, vec_spec, whole_spec, col_spec, part_spec, col_spec, part_spec, col_spec, part_spec, P('tp', None), whole_spec, col_spec, col_spec, P('tp', None), whole_spec, P('tp', None))
    out_specs = (row_spec, cache_spec, cache_spec, vec_spec, vec_spec)
    return jax.shard_map(local_step, mesh=mesh, in_specs=in_specs, out_specs=out_specs, check_vma=False)
```

time: 235 us -> 105 us (0.45)
  Pallas kernels: 0 us -> 94.3 us
  waiting for transfers between devices: 92.6 us -> 0 us
  matrix products: 69.1 us -> 0 us
  other arithmetic: 44.8 us -> 0 us
  between operations: 14.3 us -> 0.65 us
  blocking collectives: 11 us -> 0 us
  local copies, waits for them, and re-layouts: 2.16 us -> 9.83 us
    pallas_call x0 -> x2, Pallas kernels: none -> 94.3 us  [the longest x1 67.3 us: tail_call(): pl.pallas_call(tail_kernel, out_shape=(jax.ShapeDtypeStruct((BATCH, D), b...]
    psum x2 -> x0, waiting for transfers between devices: 92.6 us -> none  [the longest x1 48 us: local_step(): attn_sum = lax.psum(attn_part, 'tp')]
    dot_general x8 -> x0, matrix products: 60.8 us -> none  [the longest x1 33.8 us: local_step(): lax.dot_general(final_norm, w_head, (((1,), (1,)), ((), ())), preferred_e...]
    select_n x1 -> x0, other arithmetic: 24 us -> none  [attention_block(): k_all = jnp.where(write_mask, k_new[:, None], k_cache)]
    reduce_sum x5 -> x0, other arithmetic: 13 us -> none  [the longest x1 8.05 us: local_step(): local_sum = jnp.sum(jnp.exp(logits - local_max[:, None]), axis=1)]
    all_gather x1 -> x0, blocking collectives: 11 us -> none  [local_step(): lax.all_gather(jnp.stack([local_max, local_sum, local_target]), 'tp')]
    sub x1 -> x0, matrix products: 8.29 us -> none  [attention_block(): exp_scores = jnp.exp(scores - row_max)]
    reshape x0 -> x4, local copies, waits for them, and re-layouts: none -> 5.08 us  [the longest x1 1.29 us: local_step(): g_final.reshape(1, D)]
  transfers between devices with their start and end apart: 2 -> 0, of which waited for: 2 -> 0; matrix products, arithmetic and copies ran while one was open for 0% -> 0% of each run, Pallas kernels for 0% -> 0%
where the time goes in v1:
time: 105 us
  Pallas kernels  94.3 us (90%)
  local copies, waits for them, and re-layouts  9.83 us (9%)
    pallas_call x1, Pallas kernels, tail_call(): pl.pallas_call(tail_kernel, out_shape=(jax.ShapeDtypeStruct((BATCH, D), b...  67.3 us
    pallas_call x1, Pallas kernels, attn_call(): pl.pallas_call(attn_kernel, out_shape=(cache, cache, jax.ShapeDtypeStruct...  27 us
    unnamed x3, local copies, waits for them, and re-layouts  4.76 us

profile of v1, /device:TPU:0, one launch (start us, length us, event | category | flops | bytes accessed | tf_op | source)
XLA Modules:
  0.0 104.8 jit_solution(647484141635419818)
XLA Ops:
  0.6 1.2 %reshape.56.bq_hbm = bf16[1,256]{1,0:T(2,128)(2,1)} reshape(bf16[256]{0:T(256)(128)(2,1)} %param.26) | data formatting | bytes 1024 | tf_op jit(solution)/shard_map/reshape | solution.py:468
  1.9 1.3 %reshape.55.g_hbm = bf16[1,2048]{1,0:T(2,128)(2,1)} reshape(bf16[2048]{0:T(1024)(128)(2,1)} %param.24) | data formatting | bytes 8192 | tf_op jit(solution)/shard_map/reshape | solution.py:468
  3.1 1.3 %reshape.60.gm_ref = bf16[1,2048]{1,0:T(2,128)(2,1)} reshape(bf16[2048]{0:T(1024)(128)(2,1)} %param.32) | data formatting | bytes 8192 | tf_op jit(solution)/shard_map/reshape | solution.py:470
  4.4 1.3 %reshape.61.gf_ref = bf16[1,2048]{1,0:T(2,128)(2,1)} reshape(bf16[2048]{0:T(1024)(128)(2,1)} %param.36) | data formatting | bytes 8192 | tf_op jit(solution)/shard_map/reshape | solution.py:470
  5.7 27.0 %attn.1 = (bf16[16384,512]{1,0:T(8,128)(2,1)}, bf16[16384,512]{1,0:T(8,128)(2,1)}, bf16[2,4,256,256]{3,2,1,0:T(8,128)(2,1)}) custom-call(s32[256]{0:T(256)} %len_s.1, bf16[256,2048]{1,0:T(8,128)(2,1)} %x_hbm.3, s32[1,256]{1,0:T(1,128)} %bitcast.28, bf16[16384,512]{1,0:T(8,128)(2,1)} %bitcast.24, bf16[16384,512]{1,0:T(8,128)(2,1)} %bitcast.25, ...), custom_call_target="tpu_custom_call" | custom-call | flops 10000000000 | bytes 73400320 | tf_op jit(solution)/shard_map/attn/pallas_call | solution.py:180
  32.7 67.3 %tail.1 = (bf16[256,2048]{1,0:T(8,128)(2,1)}, f32[1,256]{1,0:T(1,128)}, f32[1,256]{1,0:T(1,128)}) custom-call(bf16[2,4,256,256]{3,2,1,0:T(8,128)(2,1)} %get-tuple-element.11.part_ref, bf16[256,2048]{1,0:T(8,128)(2,1)} %x_hbm.3, s32[1,256]{1,0:T(1,128)} %bitcast.29, bf16[1,2048]{1,0:T(2,128)(2,1)} %reshape.60.gm_ref, bf16[1,2048]{1,0:T(2,128)(2,1)} %reshape.61.gf_ref, ...), custom_call_target="tpu_custom_call" | custom-call | flops 20000000000 | bytes 83886080 | tf_op jit(solution)/shard_map/tail/pallas_call | solution.py:440
  100.0 2.3 %copy.29 = bf16[256,2048]{1,0:T(8,128)(2,1)} copy(bf16[256,2048]{1,0:T(8,128)(2,1)} %get-tuple-element.22) | data formatting | bytes 2097152
  102.4 1.2 %copy.30 = f32[256]{0:T(256)} copy(f32[256]{0:T(256)} %bitcast.31) | data formatting | bytes 2048
  103.6 1.2 %copy.31 = f32[256]{0:T(256)} copy(f32[256]{0:T(256)} %bitcast.30) | data formatting | bytes 2048

commit v2 on v1

v2 whole, which is shorter than its diff:
```python
import functools
import math

import jax
import jax.numpy as jnp
from jax import lax
from jax.experimental import pallas as pl
from jax.experimental.pallas import tpu as pltpu
from jax.sharding import PartitionSpec as P

THETA = 1000000.0
EPS = 1e-6
BATCH = 256
LMAX = 512
D = 2048
HEAD = 64
FF = 1024
STEP = 16
NSTEP = BATCH // STEP
BLK = STEP * HEAD
NPAIR = NSTEP // 2
HOLD = 2
COL = D // 8
HALF = BATCH // 2
VOC = 16032
VCH = 1024
NFULL = VOC // VCH
VTAIL = VOC - NFULL * VCH
NRING = 7
SUB = 256
GROUP = 3

f32 = jnp.float32
bf16 = jnp.bfloat16
NT = (((1,), (1,)), ((), ()))
MESH = pl.DeviceIdType.MESH


def iota(shape, dim):
    return lax.broadcasted_iota(jnp.int32, shape, dim)


def row_of(ref, start, count):
    return jnp.concatenate([ref[start + i:start + i + 1, :] for i in range(count)], axis=1).astype(f32)


def inverse_rms(pieces):
    squares = [piece * piece for piece in pieces]
    while len(squares) > 1:
        squares = [squares[i] + squares[i + 1] for i in range(0, len(squares), 2)]
    return lax.rsqrt(jnp.sum(squares[0], axis=-1, keepdims=True) * (1.0 / D) + EPS)


def attn_kernel(len_s, x_hbm, len_hbm, k_hbm, v_hbm, g_hbm, wq_hbm, bq_hbm, wk_hbm, bk_hbm, wv_hbm, bv_hbm, wo_hbm,
                ko_hbm, vo_hbm, part_ref,
                x_v, len_v, g_v, wq_v, bq_v, wkv_v, bk_v, bv_v, wo_v, kbuf0, kbuf1, vbuf0, vbuf1, normed, knv, qdup, lenc, attn,
                in_sem, rd_sem, wr_sem):
    def load(src, dst, n):
        copy = pltpu.make_async_copy(src, dst, in_sem.at[n])
        copy.start()
        return copy

    scope = jax.named_scope
    small = [
        load(x_hbm, x_v, 0),
        load(g_hbm, g_v, 1),
        load(len_hbm, len_v, 2),
        load(wk_hbm, wkv_v.at[pl.ds(0, HEAD)], 3),
        load(wv_hbm, wkv_v.at[pl.ds(HEAD, HEAD)], 4),
        load(bk_hbm, bk_v, 5),
        load(bv_hbm, bv_v, 6),
        load(wq_hbm, wq_v, 7),
        load(bq_hbm, bq_v, 8),
    ]

    kbuf, vbuf = (kbuf0, kbuf1), (vbuf0, vbuf1)

    def reads(p, j):
        rows = pl.ds((2 * j + p) * BLK, BLK)
        return (pltpu.make_async_copy(k_hbm.at[rows], kbuf[p].at[j], rd_sem.at[p, j]),
                pltpu.make_async_copy(v_hbm.at[rows], vbuf[p].at[j], rd_sem.at[2 + p, j]))

    def writes(p, j):
        rows = pl.ds((2 * j + p) * BLK, BLK)
        return (pltpu.make_async_copy(kbuf[p].at[j], ko_hbm.at[rows], wr_sem.at[p, j]),
                pltpu.make_async_copy(vbuf[p].at[j], vo_hbm.at[rows], wr_sem.at[2 + p, j]))

    def start(copies):
        for copy in copies:
            copy.start()

    def wait(copies):
        for copy in copies:
            copy.wait()

    start(reads(0, 0))
    start(reads(1, 0))
    with scope("loads"):
        for copy in small:
            copy.wait()
    for j in range(1, NPAIR):
        start(reads(0, j))
        start(reads(1, j))
    wo_copy = load(wo_hbm, wo_v, 9)

    @pl.loop(0, BATCH // 32)
    @scope("norm")
    def _(r):
        rows = pl.ds(pl.multiple_of(r * 32, 32), 32)
        xs = [x_v[rows, d * 128:(d + 1) * 128].astype(f32) for d in range(16)]
        inv = inverse_rms(xs)
        for d in range(16):
            normed[rows, d * 128:(d + 1) * 128] = (xs[d] * inv * row_of(g_v, d, 1)).astype(bf16)

    freq = jnp.exp(iota((HEAD // 2, BATCH), 0).astype(f32) * (-2.0 / HEAD * math.log(THETA)))
    angles = jnp.broadcast_to(len_v[...].astype(f32), (HEAD // 2, BATCH)) * freq
    cos_t = jnp.cos(angles)
    sin_t = jnp.sin(angles)
    cos_q = jnp.concatenate([cos_t] * 4, axis=0).T
    sin_q = jnp.concatenate([sin_t] * 4, axis=0).T
    lenc[...] = jnp.broadcast_to(len_v[...], (128, BATCH)).astype(f32).T

    bias = jnp.concatenate([bk_v[...].astype(f32), bv_v[...].astype(f32)], axis=1)
    bias = jnp.broadcast_to(bias, (128, 128)).T
    bias = jnp.concatenate([bias, bias], axis=1)
    kv = lax.dot_general(wkv_v[...], normed[...], NT, preferred_element_type=f32) + bias
    first, second = kv[:HEAD // 2], kv[HEAD // 2:HEAD]
    kv = jnp.concatenate([first * cos_t - second * sin_t, second * cos_t + first * sin_t, kv[HEAD:]], axis=0)
    kv = kv.astype(bf16).astype(f32)
    for i in range(NSTEP):
        part = kv[:, (i // 8) * 128:(i // 8) * 128 + 128]
        shift = (128 - STEP * (i % 8)) % 128
        knv[i] = pltpu.roll(part, shift, 1) if shift else part

    q = jnp.dot(normed[...], wq_v[...], preferred_element_type=f32) + row_of(bq_v, 0, 2)
    lane = iota((BATCH, 128), 1)
    low = lane < HEAD
    early = lax.rem(lane, HEAD) < HEAD // 2
    for j in range(2):
        qa = q[:, j * 128:j * 128 + 128]
        rot = jnp.where(early, -pltpu.roll(qa, 96, 1), pltpu.roll(qa, 32, 1))
        qa = qa * cos_q + rot * sin_q
        swap = pltpu.roll(qa, HEAD, 1)
        qdup[2 * j] = jnp.where(low, qa, swap).astype(bf16)
        qdup[2 * j + 1] = jnp.where(low, swap, qa).astype(bf16)

    def update(p, j):
        i = 2 * j + p
        lane_l = iota((HEAD, LMAX), 1)
        fresh = knv[i]
        for s in range(STEP):
            here = lane_l == len_s[i * STEP + s]
            rows = pl.ds(s * HEAD, HEAD)
            kcol = jnp.broadcast_to(fresh[:HEAD, s:s + 1], (HEAD, LMAX)).astype(bf16)
            vcol = jnp.broadcast_to(fresh[HEAD:, s:s + 1], (HEAD, LMAX)).astype(bf16)
            kbuf[p][j, rows, :] = jnp.where(here, kcol, kbuf[p][j, rows, :])
            vbuf[p][j, rows, :] = jnp.where(here, vcol, vbuf[p][j, rows, :])

    def attend(p, j):
        seqs = pl.ds(pl.multiple_of((2 * j + p) * STEP, STEP), STEP)
        diag = iota((STEP, BLK), 1) // HEAD == iota((STEP, BLK), 0)
        lhs = jnp.concatenate(
            [jnp.where(diag, jnp.concatenate([qdup[h, seqs, :]] * 8, axis=1), jnp.zeros((), bf16)) for h in range(4)], axis=0)
        scores = jnp.dot(lhs, kbuf[p][j], preferred_element_type=f32) * (HEAD ** -0.5)
        limit = jnp.concatenate([lenc[seqs, :]] * 4, axis=0)
        limit = jnp.concatenate([limit] * 4, axis=1)
        scores = jnp.where(iota((4 * STEP, LMAX), 1).astype(f32) <= limit, scores, -jnp.inf)
        top = jnp.max(scores, axis=-1, keepdims=True)
        expd = jnp.exp(scores - top)
        probs = (expd / jnp.sum(expd, axis=-1, keepdims=True)).astype(bf16)
        out = lax.dot_general(probs, vbuf[p][j], NT, preferred_element_type=f32)
        row_s = lax.rem(iota((4 * STEP, 128), 0), STEP)
        lane_s = iota((4 * STEP, 128), 1) // HEAD
        acc = jnp.zeros((4 * STEP, 128), f32)
        for t in range(8):
            acc = acc + jnp.where(row_s == lane_s + 2 * t, out[:, t * 128:t * 128 + 128], 0.0)
        acc = acc + pltpu.roll(acc, HEAD, 1)
        low16 = iota((STEP, 128), 1) < HEAD
        attn[seqs, :] = jnp.concatenate(
            [jnp.where(low16, acc[2 * t * STEP:(2 * t + 1) * STEP], acc[(2 * t + 1) * STEP:(2 * t + 2) * STEP]) for t in range(2)],
            axis=1).astype(bf16)

    wait(reads(0, 0))
    with scope("update"):
        update(0, 0)

    @pl.loop(0, NPAIR - 1)
    def _(j):
        with scope("kvwait"):
            wait(reads(1, j))
        with scope("pair"):
            update(1, j)
            attend(0, j)
        with scope("kvwait"):
            wait(reads(0, j + 1))
        with scope("pair"):
            update(0, j + 1)
            attend(1, j)

        @pl.when(j == HOLD)
        def _():
            for jj in range(HOLD + 1):
                start(writes(0, jj))
                start(writes(1, jj))

        @pl.when(j > HOLD)
        def _():
            start(writes(0, j))
            start(writes(1, j))

    wait(reads(1, NPAIR - 1))
    with scope("pair"):
        update(1, NPAIR - 1)
        start(writes(0, NPAIR - 1))
        start(writes(1, NPAIR - 1))
        attend(0, NPAIR - 1)
        attend(1, NPAIR - 1)

    wo_copy.wait()
    for d in range(8):
        prod = jnp.dot(attn[...], wo_v[:, d * COL:(d + 1) * COL], preferred_element_type=f32)
        part_ref[d % 2, d // 2] = prod.astype(bf16)
    with scope("drain"):
        for j in range(NPAIR):
            wait(writes(0, j))
            wait(writes(1, j))


def attn_call(lens, x, k, v, g, wq, bq, wk, bk, wv, bv, wo):
    anyspec = pl.BlockSpec(memory_space=pl.ANY)
    cache = jax.ShapeDtypeStruct((BATCH * HEAD, LMAX), bf16)
    return pl.pallas_call(
        attn_kernel,
        out_shape=(cache, cache, pltpu.VMEM((2, 4, BATCH, COL), bf16)),
        in_specs=[pl.BlockSpec(memory_space=pltpu.SMEM)] + [anyspec] * 12,
        out_specs=(anyspec, anyspec, pl.BlockSpec(memory_space=pltpu.VMEM)),
        scratch_shapes=[
            pltpu.VMEM((BATCH, D), bf16), pltpu.VMEM((1, BATCH), jnp.int32), pltpu.VMEM((16, 128), bf16),
            pltpu.VMEM((D, 4 * HEAD), bf16), pltpu.VMEM((2, 128), bf16), pltpu.VMEM((2 * HEAD, D), bf16),
            pltpu.VMEM((1, HEAD), bf16), pltpu.VMEM((1, HEAD), bf16), pltpu.VMEM((4 * HEAD, D), bf16),
            *[pltpu.VMEM((NPAIR, BLK, LMAX), bf16)] * 4,
            pltpu.VMEM((BATCH, D), bf16), pltpu.VMEM((NSTEP, 128, 128), f32), pltpu.VMEM((4, BATCH, 128), bf16),
            pltpu.VMEM((BATCH, 128), f32), pltpu.VMEM((BATCH, 4 * HEAD), bf16),
            pltpu.SemaphoreType.DMA((10,)), pltpu.SemaphoreType.DMA((4, NPAIR)), pltpu.SemaphoreType.DMA((4, NPAIR)),
        ],
        compiler_params=pltpu.CompilerParams(vmem_limit_bytes=56 * 2**20),
        cost_estimate=pl.CostEstimate(flops=10**10, bytes_accessed=70 * 2**20, transcendentals=10**6),
        name="attn",
    )(lens, x, lens.reshape(1, BATCH), k, v, g, wq, bq, wk, bk, wv, bv, wo)


def meet(me):
    barrier = pltpu.get_barrier_semaphore()
    for k in range(1, 8):
        pl.semaphore_signal(barrier, inc=1, device_id={"tp": lax.rem(me + k, 8)}, device_id_type=MESH)
    pl.semaphore_wait(barrier, 7)


def tail_kernel(part_ref, x_hbm, tok_ref, gm_ref, gf_ref, wg_hbm, wu_hbm, wd_hbm, wh_hbm,
                y_ref, out_ref,
                xown, wg_v, wu_v, wd_v, ring, part2, rs1, s2s, s2r, own, afull, yfull, mbuf, hid, fbuf, fturn, zbuf, stats, allst,
                in_sem, ring_sem, send_sem, recv_sem, st_send, st_recv):
    me = lax.axis_index("tp")
    core = lax.rem(me, 2)
    chip = me // 2
    partner = me + 1 - 2 * core
    chip_x = chip + 1 - 2 * lax.rem(chip, 2)
    chip_y = chip + 2 - 4 * (chip // 2)
    chip_d = 3 - chip
    others = (chip_x, chip_y, chip_d)

    def load(src, dst, n):
        copy = pltpu.make_async_copy(src, dst, in_sem.at[n])
        copy.start()
        return copy

    cols = pl.ds(pl.multiple_of(me * COL, COL), COL)
    xown_copy = load(x_hbm.at[:, cols], xown, 0)
    wg_copy = load(wg_hbm, wg_v, 1)
    wu_copy = load(wu_hbm, wu_v, 2)
    wd_copy = load(wd_hbm, wd_v, 3)

    def chunk(i):
        slot = lax.rem(i, NRING)
        return pltpu.make_async_copy(wh_hbm.at[pl.ds(i * VCH, VCH)], ring.at[slot], ring_sem.at[slot])

    tail_slot = NFULL % NRING
    tail_copy = pltpu.make_async_copy(wh_hbm.at[pl.ds(NFULL * VCH, VTAIL)], ring.at[tail_slot, pl.ds(0, VTAIL)],
                                      ring_sem.at[tail_slot])
    for i in range(NRING):
        chunk(i).start()

    with jax.named_scope('barrier'):
        meet(me)

    def remote(src, dst, n, dev):
        return pltpu.make_async_remote_copy(src_ref=src, dst_ref=dst, send_sem=send_sem.at[n], recv_sem=recv_sem.at[n],
                                            device_id={"tp": dev}, device_id_type=MESH)

    class Reduce:
        def __init__(self, which, half, part, full):
            self.base = (which * 2 + half) * 11
            self.which, self.half, self.part, self.full = which, half, part, full
            self.rows = pl.ds(half * HALF, HALF)

        def s1(self):
            return remote(self.part.at[1 - core, :, self.rows, :], rs1.at[self.which, self.half], self.base, partner)

        def s2(self, k):
            return remote(s2s.at[self.which, self.half, k], s2r.at[self.which, self.half, k], self.base + 1 + k,
                          2 * others[k] + core)

        def s3(self, k):
            block = self.full.at[me, self.rows]
            return remote(block, block, self.base + 4 + k, 2 * others[k] + core)

        def s3own(self):
            block = self.full.at[me, self.rows]
            return remote(block, block, self.base + 7, partner)

        def s4(self, k):
            block = self.full.at[2 * others[k] + core, self.rows]
            return remote(block, block, self.base + 8 + k, partner)

        @jax.named_scope('scatter')
        def scatter(self):
            self.s1().wait_recv()
            for k in (2, 0, 1):
                total = self.part[core, others[k], self.rows, :].astype(f32) + rs1[self.which, self.half, others[k]].astype(f32)
                s2s[self.which, self.half, k] = total.astype(bf16)
                self.s2(k).start()
            own[self.which, self.half] = (self.part[core, chip, self.rows, :].astype(f32)
                                          + rs1[self.which, self.half, chip].astype(f32))

        @jax.named_scope('gather')
        def gather(self, resid):
            for k in range(3):
                self.s2(k).wait_recv()
            total = resid + own[self.which, self.half]
            for k in range(3):
                total = total + s2r[self.which, self.half, k].astype(f32)
            self.full[me, self.rows, :] = total.astype(bf16)
            for k in (2, 0, 1):
                self.s3(k).start()
            self.s3own().start()

        @jax.named_scope('forward')
        def forward(self):
            for k in range(3):
                self.s3(k).wait_recv()
                self.s4(k).start()

        @jax.named_scope('finish')
        def finish(self):
            self.s3own().wait_recv()
            for k in range(3):
                self.s4(k).wait_recv()

        def drain(self):
            self.s1().wait_send()
            self.s3own().wait_send()
            for k in range(3):
                self.s2(k).wait_send()
                self.s3(k).wait_send()
                self.s4(k).wait_send()

    first = [Reduce(0, h, part_ref, afull) for h in range(2)]
    second = [Reduce(1, h, part2, yfull) for h in range(2)]

    @jax.named_scope('norm_rows')
    def norm_rows(full, half, gain_ref, dst, copy_to=None):
        @pl.loop(0, HALF // 32)
        def _(r):
            rows = pl.ds(pl.multiple_of(half * HALF + r * 32, 32), 32)
            xs = []
            for d in range(16):
                block = full[d // 2, rows, (d % 2) * 128:(d % 2) * 128 + 128]
                if copy_to is not None:
                    copy_to[rows, d * 128:(d + 1) * 128] = block
                xs.append(block.astype(f32))
            inv = inverse_rms(xs)
            for d in range(16):
                dst[rows, d * 128:(d + 1) * 128] = (xs[d] * inv * row_of(gain_ref, d, 1)).astype(bf16)

    @jax.named_scope('gate_up')
    def gate_up(half, between=None):
        rows = pl.ds(half * HALF, HALF)
        for n in range(4):
            if n == 3 and between is not None:
                between()
            cs = slice(n * 256, (n + 1) * 256)
            gate = jnp.dot(mbuf[rows, :], wg_v[:, cs], preferred_element_type=f32)
            up = jnp.dot(mbuf[rows, :], wu_v[:, cs], preferred_element_type=f32)
            hid[rows, cs] = (gate / (1.0 + jnp.exp(-gate)) * up).astype(bf16)

    @jax.named_scope('down')
    def down(half):
        rows = pl.ds(half * HALF, HALF)
        for d in range(8):
            prod = jnp.dot(hid[rows, :], wd_v[:, d * COL:(d + 1) * COL], preferred_element_type=f32)
            part2[d % 2, d // 2, rows, :] = prod.astype(bf16)

    for h in range(2):
        first[h].s1().start()
    for h in range(2):
        first[h].scatter()
    xown_copy.wait()
    for h in range(2):
        first[h].gather(xown[h * HALF:(h + 1) * HALF, :].astype(f32))
    first[0].forward()
    first[0].finish()
    norm_rows(afull, 0, gm_ref, mbuf)
    wg_copy.wait()
    wu_copy.wait()
    gate_up(0, first[1].forward)
    wd_copy.wait()
    down(0)
    second[0].s1().start()
    first[1].finish()
    norm_rows(afull, 1, gm_ref, mbuf)
    second[0].scatter()
    gate_up(1)
    down(1)
    second[1].s1().start()
    second[1].scatter()
    for h in range(2):
        second[h].gather(afull[me, h * HALF:(h + 1) * HALF, :].astype(f32))
    for h in range(2):
        second[h].forward()
        second[h].finish()
        norm_rows(yfull, h, gf_ref, fbuf, y_ref)
        with jax.named_scope("turn"):
            for d in range(8):
                cs = slice(d * COL, (d + 1) * COL)
                fturn[cs, h * HALF:(h + 1) * HALF] = fbuf[h * HALF:(h + 1) * HALF, cs].T

    tok = jnp.broadcast_to(tok_ref[...] - me * VOC, (8, BATCH))

    def absorb(buf, size, base, state):
        top, total, target = state
        z = zbuf[buf, pl.ds(0, size), :].reshape(size // 8, 8, BATCH)
        new_top = jnp.maximum(top, jnp.max(z, axis=0))
        total = total * jnp.exp(top - new_top) + jnp.sum(jnp.exp(z - new_top[None]), axis=0)
        hit = iota(z.shape, 0) * 8 + iota(z.shape, 1) == (tok - base)[None]
        target = target + jnp.sum(jnp.where(hit, z, 0.0), axis=0)
        return new_top, total, target

    def score(slot, size, base, state, before):
        for n, start in enumerate(range(0, size, SUB)):
            rows = min(SUB, size - start)
            z = jnp.dot(ring[slot, pl.ds(start, rows), :], fturn[...], preferred_element_type=f32)
            state = absorb((n + 1) % 2, SUB, before if n == 0 else base + start - SUB, state)
            zbuf[n % 2, pl.ds(0, rows), :] = z
        return state

    def head_step(t, state):
        with jax.named_scope('hwait'):
            for u in range(GROUP):
                chunk(t * GROUP + u).wait()
        for u in range(GROUP):
            i = t * GROUP + u
            before = jnp.where(i == 0, -2 * BATCH * VOC, i * VCH - SUB)
            state = score(lax.rem(i, NRING), VCH, i * VCH, state, before)
        for u in range(GROUP):
            nxt = t * GROUP + u + NRING

            @pl.when(nxt < NFULL)
            def _():
                chunk(nxt).start()

            @pl.when(nxt == NFULL)
            def _():
                tail_copy.start()
        return state

    zero = jnp.zeros((8, BATCH), f32)
    zbuf[1] = jnp.full((SUB, BATCH), -jnp.inf, f32)
    state = (jnp.full((8, BATCH), jnp.finfo(jnp.float32).min, f32), zero, zero)
    state = lax.fori_loop(0, NFULL // GROUP, head_step, state)
    tail_copy.wait()
    state = score(tail_slot, VTAIL, NFULL * VCH, state, NFULL * VCH - SUB)
    last = (VTAIL - 1) // SUB
    top8, total8, target8 = absorb(last % 2, VTAIL - last * SUB, NFULL * VCH + last * SUB, state)
    top = jnp.max(top8, axis=0, keepdims=True)
    total = jnp.sum(total8 * jnp.exp(top8 - top), axis=0, keepdims=True)
    target = jnp.sum(target8, axis=0, keepdims=True)
    zero = jnp.zeros((1, BATCH), f32)

    stats[...] = jnp.concatenate([top, total, target, zero, zero, zero, zero, zero], axis=0)
    allst[me] = stats[...]

    def stat_copy(k):
        return pltpu.make_async_remote_copy(src_ref=stats, dst_ref=allst.at[me], send_sem=st_send.at[k - 1],
                                            recv_sem=st_recv.at[k - 1], device_id={"tp": lax.rem(me + k, 8)},
                                            device_id_type=MESH)

    for k in range(1, 8):
        stat_copy(k).start()
    with jax.named_scope('statwait'):
        for k in range(1, 8):
            stat_copy(k).wait_recv()
    out_ref[...] = allst[...]
    for h in range(2):
        first[h].drain()
        second[h].drain()
    for k in range(1, 8):
        stat_copy(k).wait_send()


def tail_call(part, x, tok, gm, gf, wg, wu, wd, wh):
    anyspec = pl.BlockSpec(memory_space=pl.ANY)
    vspec = pl.BlockSpec(memory_space=pltpu.VMEM)
    blocks = (2, 2, 3, HALF, COL)
    return pl.pallas_call(
        tail_kernel,
        out_shape=(pltpu.VMEM((BATCH, D), bf16), pltpu.VMEM((8, 8, BATCH), f32)),
        in_specs=[vspec, anyspec, vspec, vspec, vspec, anyspec, anyspec, anyspec, anyspec],
        out_specs=(vspec, vspec),
        scratch_shapes=[
            pltpu.VMEM((BATCH, COL), bf16), pltpu.VMEM((D, FF), bf16), pltpu.VMEM((D, FF), bf16), pltpu.VMEM((FF, D), bf16),
            pltpu.VMEM((NRING, VCH, D), bf16), pltpu.VMEM((2, 4, BATCH, COL), bf16), pltpu.VMEM((2, 2, 4, HALF, COL), bf16),
            pltpu.VMEM(blocks, bf16), pltpu.VMEM(blocks, bf16), pltpu.VMEM((2, 2, HALF, COL), f32),
            pltpu.VMEM((8, BATCH, COL), bf16), pltpu.VMEM((8, BATCH, COL), bf16), pltpu.VMEM((BATCH, D), bf16),
            pltpu.VMEM((BATCH, FF), bf16), pltpu.VMEM((BATCH, D), bf16), pltpu.VMEM((D, BATCH), bf16), pltpu.VMEM((2, SUB, BATCH), f32),
            pltpu.VMEM((8, BATCH), f32), pltpu.VMEM((8, 8, BATCH), f32),
            pltpu.SemaphoreType.DMA((4,)), pltpu.SemaphoreType.DMA((NRING,)), pltpu.SemaphoreType.DMA((44,)),
            pltpu.SemaphoreType.DMA((44,)), pltpu.SemaphoreType.DMA((7,)), pltpu.SemaphoreType.DMA((7,)),
        ],
        compiler_params=pltpu.CompilerParams(collective_id=0, has_side_effects=True, vmem_limit_bytes=54 * 2**20),
        cost_estimate=pl.CostEstimate(flops=2 * 10**10, bytes_accessed=80 * 2**20, transcendentals=10**6),
        name="tail",
    )(pltpu.with_memory_space_constraint(part, pltpu.VMEM), x, tok, gm, gf, wg, wu, wd, wh)


def end_kernel(y_ref, allst, y_hbm, logp_ref, lse_ref, sem):
    copy = pltpu.make_async_copy(y_ref, y_hbm, sem)
    copy.start()
    top = allst[0, 0:1, :]
    for d in range(1, 8):
        top = jnp.maximum(top, allst[d, 0:1, :])
    total = jnp.zeros((1, BATCH), f32)
    target = jnp.zeros((1, BATCH), f32)
    for d in range(8):
        total = total + allst[d, 1:2, :] * jnp.exp(allst[d, 0:1, :] - top)
        target = target + allst[d, 2:3, :]
    lse = top + jnp.log(total)
    lse_ref[...] = lse
    logp_ref[...] = target - lse
    copy.wait()


def end_call(y, stats):
    vspec = pl.BlockSpec(memory_space=pltpu.VMEM)
    row = jax.ShapeDtypeStruct((1, BATCH), f32)
    return pl.pallas_call(
        end_kernel,
        out_shape=(jax.ShapeDtypeStruct((BATCH, D), bf16), row, row),
        in_specs=[vspec, vspec],
        out_specs=(pl.BlockSpec(memory_space=pl.ANY), vspec, vspec),
        scratch_shapes=[pltpu.SemaphoreType.DMA],
        compiler_params=pltpu.CompilerParams(vmem_limit_bytes=4 * 2**20),
        name="end",
    )(y, stats)


def local_step(x, lens, k_cache, v_cache, tok, g_attn, w_q, b_q, w_k, b_k, w_v, b_v, w_o, g_mlp, w_gate, w_up, w_down, g_final, w_head):
    def flat(cache):
        return cache.transpose(0, 2, 3, 1).reshape(BATCH * HEAD, LMAX)

    def unflat(cache):
        return cache.reshape(BATCH, 1, HEAD, LMAX).transpose(0, 3, 1, 2)

    k_new, v_new, part = attn_call(lens, x, flat(k_cache), flat(v_cache), g_attn.reshape(16, 128), w_q, b_q.reshape(2, 128),
                                   w_k.T, b_k.reshape(1, -1), w_v.T, b_v.reshape(1, -1), w_o)
    y, logp, lse = end_call(*tail_call(part, x, tok.reshape(1, BATCH), g_mlp.reshape(16, 128), g_final.reshape(16, 128), w_gate, w_up, w_down, w_head))
    return y, unflat(k_new), unflat(v_new), logp.reshape(BATCH), lse.reshape(BATCH)


def solution(mesh):
    row_spec = P('dp', None)
    vec_spec = P('dp')
    cache_spec = P('dp', None, 'tp', None)
    col_spec = P(None, 'tp')
    part_spec = P('tp')
    whole_spec = P(None)
    in_specs = (row_spec, vec_spec, cache_spec, cache_spec, vec_spec, whole_spec, col_spec, part_spec, col_spec, part_spec, col_spec, part_spec, P('tp', None), whole_spec, col_spec, col_spec, P('tp', None), whole_spec, P('tp', None))
    out_specs = (row_spec, cache_spec, cache_spec, vec_spec, vec_spec)
    return jax.shard_map(local_step, mesh=mesh, in_specs=in_specs, out_specs=out_specs, check_vma=False)
```

time: 105 us -> 87 us (0.83)
  local copies, waits for them, and re-layouts: 9.83 us -> 0 us
  Pallas kernels: 94.3 us -> 86 us
    pallas_call x2 -> x3, Pallas kernels: 94.3 us -> 86 us  [the longest x1 61.6 us: tail_call(): pl.pallas_call(tail_kernel, out_shape=(pltpu.VMEM((BATCH, D), bf16), pltp...]
    reshape x4 -> x0, local copies, waits for them, and re-layouts: 5.08 us -> none  [the longest x1 1.29 us: local_step(): g_final.reshape(1, D)]
    unnamed x3 -> x0, local copies, waits for them, and re-layouts: 4.76 us -> none
where the time goes in v2:
time: 87 us; the launch traced here: 86.8 us
  Pallas kernels  86 us (99%)
    pallas_call x1, Pallas kernels, tail_call(): pl.pallas_call(tail_kernel, out_shape=(pltpu.VMEM((BATCH, D), bf16), pltp...  61.6 us
    pallas_call x1, Pallas kernels, attn_call(): pl.pallas_call(attn_kernel, out_shape=(cache, cache, pltpu.VMEM((2, 4, BA...  22.8 us

profile of v2, /device:TPU:0, one launch (start us, length us, event | category | flops | bytes accessed | tf_op | source)
XLA Modules:
  0.0 86.8 jit_solution(9615913624609490699)
XLA Ops:
  0.6 22.8 %attn.1 = (bf16[16384,512]{1,0:T(8,128)(2,1)}, bf16[16384,512]{1,0:T(8,128)(2,1)}, bf16[2,4,256,256]{3,2,1,0:T(8,128)(2,1)S(1)}) custom-call(s32[256]{0:T(256)} %len_s.1, bf16[256,2048]{1,0:T(8,128)(2,1)} %x_hbm.3, s32[1,256]{1,0:T(1,128)} %bitcast.32, bf16[16384,512]{1,0:T(8,128)(2,1)} %bitcast.28, bf16[16384,512]{1,0:T(8,128)(2,1)} %bitcast.29, ...), custom_call_target="tpu_custom_call" | custom-call | flops 10000000000 | bytes 73400320 | tf_op jit(solution)/shard_map/attn/pallas_call | solution.py:232
  23.5 61.6 %tail.1 = (bf16[256,2048]{1,0:T(8,128)(2,1)S(1)}, f32[8,8,256]{2,1,0:T(8,128)S(1)}) custom-call(bf16[2,4,256,256]{3,2,1,0:T(8,128)(2,1)S(1)} %get-tuple-element.13.part_ref, bf16[256,2048]{1,0:T(8,128)(2,1)} %x_hbm.3, s32[1,256]{1,0:T(1,128)} %bitcast.36, bf16[16,128]{1,0:T(8,128)(2,1)} %bitcast.34, bf16[16,128]{1,0:T(8,128)(2,1)} %bitcast.35, ...), custom_call_target="tpu_custom_call" | custom-call | flops 20000000000 | bytes 83886080 | tf_op jit(solution)/shard_map/tail/pallas_call | solution.py:514
  85.1 1.5 %end.1 = (bf16[256,2048]{1,0:T(8,128)(2,1)}, f32[1,256]{1,0:T(1,128)}, f32[1,256]{1,0:T(1,128)}) custom-call(bf16[256,2048]{1,0:T(8,128)(2,1)S(1)} %get-tuple-element.14.y_ref, f32[8,8,256]{2,1,0:T(8,128)S(1)} %get-tuple-element.15.allst), custom_call_target="tpu_custom_call" | custom-call | tf_op jit(solution)/shard_map/end/pallas_call | solution.py:555

commit v3 on v2

--- a/solution.py
+++ b/solution.py
@@ -22,6 +22,8 @@
 HOLD = 2
 COL = D // 8
 HALF = BATCH // 2
+NMSG = 11
+AT = 1
 VOC = 16032
 VCH = 1024
 NFULL = VOC // VCH
@@ -267,7 +269,6 @@
     chip_x = chip + 1 - 2 * lax.rem(chip, 2)
     chip_y = chip + 2 - 4 * (chip // 2)
     chip_d = 3 - chip
-    others = (chip_x, chip_y, chip_d)
 
     def load(src, dst, n):
         copy = pltpu.make_async_copy(src, dst, in_sem.at[n])
@@ -297,9 +298,11 @@
         return pltpu.make_async_remote_copy(src_ref=src, dst_ref=dst, send_sem=send_sem.at[n], recv_sem=recv_sem.at[n],
                                             device_id={"tp": dev}, device_id_type=MESH)
 
+    others = (chip_x, chip_y, chip_d)
+
     class Reduce:
         def __init__(self, which, half, part, full):
-            self.base = (which * 2 + half) * 11
+            self.base = (which * 2 + half) * NMSG
             self.which, self.half, self.part, self.full = which, half, part, full
             self.rows = pl.ds(half * HALF, HALF)
 
@@ -356,11 +359,14 @@
             for k in range(3):
                 self.s4(k).wait_recv()
 
-        def drain(self):
+        def drain_scatter(self):
             self.s1().wait_send()
+            for k in range(3):
+                self.s2(k).wait_send()
+
+        def drain_gather(self):
             self.s3own().wait_send()
             for k in range(3):
-                self.s2(k).wait_send()
                 self.s3(k).wait_send()
                 self.s4(k).wait_send()
 
@@ -383,22 +389,29 @@
                 dst[rows, d * 128:(d + 1) * 128] = (xs[d] * inv * row_of(gain_ref, d, 1)).astype(bf16)
 
     @jax.named_scope('gate_up')
-    def gate_up(half, between=None):
+    def gate_up(half, between):
         rows = pl.ds(half * HALF, HALF)
         for n in range(4):
-            if n == 3 and between is not None:
-                between()
+            if n in between:
+                between[n]()
             cs = slice(n * 256, (n + 1) * 256)
             gate = jnp.dot(mbuf[rows, :], wg_v[:, cs], preferred_element_type=f32)
             up = jnp.dot(mbuf[rows, :], wu_v[:, cs], preferred_element_type=f32)
             hid[rows, cs] = (gate / (1.0 + jnp.exp(-gate)) * up).astype(bf16)
 
     @jax.named_scope('down')
-    def down(half):
+    def down(half, after):
         rows = pl.ds(half * HALF, HALF)
-        for d in range(8):
-            prod = jnp.dot(hid[rows, :], wd_v[:, d * COL:(d + 1) * COL], preferred_element_type=f32)
-            part2[d % 2, d // 2, rows, :] = prod.astype(bf16)
+
+        def product(c, q):
+            d = (2 * q + c) * COL
+            return jnp.dot(hid[rows, :], wd_v[:, pl.ds(pl.multiple_of(d, COL), COL)], preferred_element_type=f32).astype(bf16)
+
+        for q in range(4):
+            part2[1 - core, q, rows, :] = product(1 - core, q)
+        after.s1().start()
+        for q in range(4):
+            part2[core, q, rows, :] = product(core, q)
 
     for h in range(2):
         first[h].s1().start()
@@ -412,19 +425,21 @@
     norm_rows(afull, 0, gm_ref, mbuf)
     wg_copy.wait()
     wu_copy.wait()
-    gate_up(0, first[1].forward)
+    gate_up(0, {3: first[1].forward})
     wd_copy.wait()
-    down(0)
-    second[0].s1().start()
+    down(0, second[0])
+    for h in range(2):
+        first[h].drain_scatter()
     first[1].finish()
     norm_rows(afull, 1, gm_ref, mbuf)
-    second[0].scatter()
-    gate_up(1)
-    down(1)
-    second[1].s1().start()
+    gate_up(1, {AT: second[0].scatter})
+    down(1, second[1])
     second[1].scatter()
     for h in range(2):
         second[h].gather(afull[me, h * HALF:(h + 1) * HALF, :].astype(f32))
+    for h in range(2):
+        first[h].drain_gather()
+        second[h].drain_scatter()
     for h in range(2):
         second[h].forward()
         second[h].finish()
@@ -497,14 +512,13 @@
     for k in range(1, 8):
         stat_copy(k).start()
     with jax.named_scope('statwait'):
+        for h in range(2):
+            second[h].drain_gather()
         for k in range(1, 8):
             stat_copy(k).wait_recv()
+        for k in range(1, 8):
+            stat_copy(k).wait_send()
     out_ref[...] = allst[...]
-    for h in range(2):
-        first[h].drain()
-        second[h].drain()
-    for k in range(1, 8):
-        stat_copy(k).wait_send()
 
 
 def tail_call(part, x, tok, gm, gf, wg, wu, wd, wh):
@@ -523,8 +537,8 @@
             pltpu.VMEM((8, BATCH, COL), bf16), pltpu.VMEM((8, BATCH, COL), bf16), pltpu.VMEM((BATCH, D), bf16),
             pltpu.VMEM((BATCH, FF), bf16), pltpu.VMEM((BATCH, D), bf16), pltpu.VMEM((D, BATCH), bf16), pltpu.VMEM((2, SUB, BATCH), f32),
             pltpu.VMEM((8, BATCH), f32), pltpu.VMEM((8, 8, BATCH), f32),
-            pltpu.SemaphoreType.DMA((4,)), pltpu.SemaphoreType.DMA((NRING,)), pltpu.SemaphoreType.DMA((44,)),
-            pltpu.SemaphoreType.DMA((44,)), pltpu.SemaphoreType.DMA((7,)), pltpu.SemaphoreType.DMA((7,)),
+            pltpu.SemaphoreType.DMA((4,)), pltpu.SemaphoreType.DMA((NRING,)), pltpu.SemaphoreType.DMA((4 * NMSG,)),
+            pltpu.SemaphoreType.DMA((4 * NMSG,)), pltpu.SemaphoreType.DMA((7,)), pltpu.SemaphoreType.DMA((7,)),
         ],
         compiler_params=pltpu.CompilerParams(collective_id=0, has_side_effects=True, vmem_limit_bytes=54 * 2**20),
         cost_estimate=pl.CostEstimate(flops=2 * 10**10, bytes_accessed=80 * 2**20, transcendentals=10**6),
@@ -532,9 +546,9 @@
     )(pltpu.with_memory_space_constraint(part, pltpu.VMEM), x, tok, gm, gf, wg, wu, wd, wh)
 
 
-def end_kernel(y_ref, allst, y_hbm, logp_ref, lse_ref, sem):
-    copy = pltpu.make_async_copy(y_ref, y_hbm, sem)
-    copy.start()
+def end_kernel(y_ref, allst, y_hbm, logp_hbm, lse_hbm, rows_v, sem):
+    copies = [pltpu.make_async_copy(y_ref, y_hbm, sem.at[0])]
+    copies[0].start()
     top = allst[0, 0:1, :]
     for d in range(1, 8):
         top = jnp.maximum(top, allst[d, 0:1, :])
@@ -544,9 +558,13 @@
         total = total + allst[d, 1:2, :] * jnp.exp(allst[d, 0:1, :] - top)
         target = target + allst[d, 2:3, :]
     lse = top + jnp.log(total)
-    lse_ref[...] = lse
-    logp_ref[...] = target - lse
-    copy.wait()
+    rows_v[0] = target - lse
+    rows_v[1] = lse
+    for n, dst in enumerate((logp_hbm, lse_hbm)):
+        copies.append(pltpu.make_async_copy(rows_v.at[n], dst, sem.at[1 + n]))
+        copies[-1].start()
+    for copy in copies:
+        copy.wait()
 
 
 def end_call(y, stats):
@@ -556,8 +574,8 @@
         end_kernel,
         out_shape=(jax.ShapeDtypeStruct((BATCH, D), bf16), row, row),
         in_specs=[vspec, vspec],
-        out_specs=(pl.BlockSpec(memory_space=pl.ANY), vspec, vspec),
-        scratch_shapes=[pltpu.SemaphoreType.DMA],
+        out_specs=(pl.BlockSpec(memory_space=pltpu.HBM),) * 3,
+        scratch_shapes=[pltpu.VMEM((2, 1, BATCH), f32), pltpu.SemaphoreType.DMA((3,))],
         compiler_params=pltpu.CompilerParams(vmem_limit_bytes=4 * 2**20),
         name="end",
     )(y, stats)

time: 87 us -> 86.2 us (level)
  no operation moved by 1% of the time
where the time goes in v3:
time: 86.2 us; the launch traced here: 86 us
  Pallas kernels  85.2 us (99%)
    pallas_call x1, Pallas kernels, tail_call(): pl.pallas_call(tail_kernel, out_shape=(pltpu.VMEM((BATCH, D), bf16), pltp...  61.4 us
    pallas_call x1, Pallas kernels, attn_call(): pl.pallas_call(attn_kernel, out_shape=(cache, cache, pltpu.VMEM((2, 4, BA...  22.8 us

profile of v3, /device:TPU:0, one launch (start us, length us, event | category | flops | bytes accessed | tf_op | source)
XLA Modules:
  0.0 86.0 jit_solution(5170069758165235136)
XLA Ops:
  0.6 22.8 %attn.1 = (bf16[16384,512]{1,0:T(8,128)(2,1)}, bf16[16384,512]{1,0:T(8,128)(2,1)}, bf16[2,4,256,256]{3,2,1,0:T(8,128)(2,1)S(1)}) custom-call(s32[256]{0:T(256)} %len_s.1, bf16[256,2048]{1,0:T(8,128)(2,1)} %x_hbm.3, s32[1,256]{1,0:T(1,128)} %bitcast.32, bf16[16384,512]{1,0:T(8,128)(2,1)} %bitcast.28, bf16[16384,512]{1,0:T(8,128)(2,1)} %bitcast.29, ...), custom_call_target="tpu_custom_call" | custom-call | flops 10000000000 | bytes 73400320 | tf_op jit(solution)/shard_map/attn/pallas_call | solution.py:234
  23.5 61.4 %tail.1 = (bf16[256,2048]{1,0:T(8,128)(2,1)S(1)}, f32[8,8,256]{2,1,0:T(8,128)S(1)}) custom-call(bf16[2,4,256,256]{3,2,1,0:T(8,128)(2,1)S(1)} %get-tuple-element.13.part_ref, bf16[256,2048]{1,0:T(8,128)(2,1)} %x_hbm.3, s32[1,256]{1,0:T(1,128)} %bitcast.36, bf16[16,128]{1,0:T(8,128)(2,1)} %bitcast.34, bf16[16,128]{1,0:T(8,128)(2,1)} %bitcast.35, ...), custom_call_target="tpu_custom_call" | custom-call | flops 20000000000 | bytes 83886080 | tf_op jit(solution)/shard_map/tail/pallas_call | solution.py:528
  84.9 1.0 %end.1 = (bf16[256,2048]{1,0:T(8,128)(2,1)}, f32[1,256]{1,0:T(1,128)}, f32[1,256]{1,0:T(1,128)}) custom-call(bf16[256,2048]{1,0:T(8,128)(2,1)S(1)} %get-tuple-element.14.y_ref, f32[8,8,256]{2,1,0:T(8,128)S(1)} %get-tuple-element.15.allst), custom_call_target="tpu_custom_call" | custom-call | tf_op jit(solution)/shard_map/end/pallas_call | solution.py:573

commit v4 on v3

--- a/solution.py
+++ b/solution.py
@@ -53,9 +53,9 @@
     return lax.rsqrt(jnp.sum(squares[0], axis=-1, keepdims=True) * (1.0 / D) + EPS)
 
 
-def attn_kernel(len_s, x_hbm, len_hbm, k_hbm, v_hbm, g_hbm, wq_hbm, bq_hbm, wk_hbm, bk_hbm, wv_hbm, bv_hbm, wo_hbm,
+def attn_kernel(len1_hbm, x_hbm, len_hbm, k_hbm, v_hbm, g_hbm, wq_hbm, bq_hbm, wk_hbm, bk_hbm, wv_hbm, bv_hbm, wo_hbm,
                 ko_hbm, vo_hbm, part_ref,
-                x_v, len_v, g_v, wq_v, bq_v, wkv_v, bk_v, bv_v, wo_v, kbuf0, kbuf1, vbuf0, vbuf1, normed, knv, qdup, lenc, attn,
+                len_s, x_v, len_v, g_v, wq_v, bq_v, wkv_v, bk_v, bv_v, wo_v, kbuf0, kbuf1, vbuf0, vbuf1, normed, knv, qdup, lenc, attn,
                 in_sem, rd_sem, wr_sem):
     def load(src, dst, n):
         copy = pltpu.make_async_copy(src, dst, in_sem.at[n])
@@ -73,6 +73,7 @@
         load(bv_hbm, bv_v, 6),
         load(wq_hbm, wq_v, 7),
         load(bq_hbm, bq_v, 8),
+        load(len1_hbm, len_s, 10),
     ]
 
     kbuf, vbuf = (kbuf0, kbuf1), (vbuf0, vbuf1)
@@ -234,16 +235,17 @@
     return pl.pallas_call(
         attn_kernel,
         out_shape=(cache, cache, pltpu.VMEM((2, 4, BATCH, COL), bf16)),
-        in_specs=[pl.BlockSpec(memory_space=pltpu.SMEM)] + [anyspec] * 12,
+        in_specs=[anyspec] * 13,
         out_specs=(anyspec, anyspec, pl.BlockSpec(memory_space=pltpu.VMEM)),
         scratch_shapes=[
+            pltpu.SMEM((BATCH,), jnp.int32),
             pltpu.VMEM((BATCH, D), bf16), pltpu.VMEM((1, BATCH), jnp.int32), pltpu.VMEM((16, 128), bf16),
             pltpu.VMEM((D, 4 * HEAD), bf16), pltpu.VMEM((2, 128), bf16), pltpu.VMEM((2 * HEAD, D), bf16),
             pltpu.VMEM((1, HEAD), bf16), pltpu.VMEM((1, HEAD), bf16), pltpu.VMEM((4 * HEAD, D), bf16),
             *[pltpu.VMEM((NPAIR, BLK, LMAX), bf16)] * 4,
             pltpu.VMEM((BATCH, D), bf16), pltpu.VMEM((NSTEP, 128, 128), f32), pltpu.VMEM((4, BATCH, 128), bf16),
             pltpu.VMEM((BATCH, 128), f32), pltpu.VMEM((BATCH, 4 * HEAD), bf16),
-            pltpu.SemaphoreType.DMA((10,)), pltpu.SemaphoreType.DMA((4, NPAIR)), pltpu.SemaphoreType.DMA((4, NPAIR)),
+            pltpu.SemaphoreType.DMA((11,)), pltpu.SemaphoreType.DMA((4, NPAIR)), pltpu.SemaphoreType.DMA((4, NPAIR)),
         ],
         compiler_params=pltpu.CompilerParams(vmem_limit_bytes=56 * 2**20),
         cost_estimate=pl.CostEstimate(flops=10**10, bytes_accessed=70 * 2**20, transcendentals=10**6),
@@ -258,9 +260,9 @@
     pl.semaphore_wait(barrier, 7)
 
 
-def tail_kernel(part_ref, x_hbm, tok_ref, gm_ref, gf_ref, wg_hbm, wu_hbm, wd_hbm, wh_hbm,
+def tail_kernel(part_ref, x_hbm, tok_hbm, gm_hbm, gf_hbm, wg_hbm, wu_hbm, wd_hbm, wh_hbm,
                 y_ref, out_ref,
-                xown, wg_v, wu_v, wd_v, ring, part2, rs1, s2s, s2r, own, afull, yfull, mbuf, hid, fbuf, fturn, zbuf, stats, allst,
+                tok_ref, gm_ref, gf_ref, xown, wg_v, wu_v, wd_v, ring, part2, rs1, s2s, s2r, own, afull, yfull, mbuf, hid, fbuf, fturn, zbuf, stats, allst,
                 in_sem, ring_sem, send_sem, recv_sem, st_send, st_recv):
     me = lax.axis_index("tp")
     core = lax.rem(me, 2)
@@ -277,6 +279,7 @@
 
     cols = pl.ds(pl.multiple_of(me * COL, COL), COL)
     xown_copy = load(x_hbm.at[:, cols], xown, 0)
+    gains = [load(gm_hbm, gm_ref, 4), load(gf_hbm, gf_ref, 5), load(tok_hbm, tok_ref, 6)]
     wg_copy = load(wg_hbm, wg_v, 1)
     wu_copy = load(wu_hbm, wu_v, 2)
     wd_copy = load(wd_hbm, wd_v, 3)
@@ -418,6 +421,8 @@
     for h in range(2):
         first[h].scatter()
     xown_copy.wait()
+    for copy in gains:
+        copy.wait()
     for h in range(2):
         first[h].gather(xown[h * HALF:(h + 1) * HALF, :].astype(f32))
     first[0].forward()
@@ -528,16 +533,17 @@
     return pl.pallas_call(
         tail_kernel,
         out_shape=(pltpu.VMEM((BATCH, D), bf16), pltpu.VMEM((8, 8, BATCH), f32)),
-        in_specs=[vspec, anyspec, vspec, vspec, vspec, anyspec, anyspec, anyspec, anyspec],
+        in_specs=[vspec] + [anyspec] * 8,
         out_specs=(vspec, vspec),
         scratch_shapes=[
+            pltpu.VMEM((1, BATCH), jnp.int32), pltpu.VMEM((16, 128), bf16), pltpu.VMEM((16, 128), bf16),
             pltpu.VMEM((BATCH, COL), bf16), pltpu.VMEM((D, FF), bf16), pltpu.VMEM((D, FF), bf16), pltpu.VMEM((FF, D), bf16),
             pltpu.VMEM((NRING, VCH, D), bf16), pltpu.VMEM((2, 4, BATCH, COL), bf16), pltpu.VMEM((2, 2, 4, HALF, COL), bf16),
             pltpu.VMEM(blocks, bf16), pltpu.VMEM(blocks, bf16), pltpu.VMEM((2, 2, HALF, COL), f32),
             pltpu.VMEM((8, BATCH, COL), bf16), pltpu.VMEM((8, BATCH, COL), bf16), pltpu.VMEM((BATCH, D), bf16),
             pltpu.VMEM((BATCH, FF), bf16), pltpu.VMEM((BATCH, D), bf16), pltpu.VMEM((D, BATCH), bf16), pltpu.VMEM((2, SUB, BATCH), f32),
             pltpu.VMEM((8, BATCH), f32), pltpu.VMEM((8, 8, BATCH), f32),
-            pltpu.SemaphoreType.DMA((4,)), pltpu.SemaphoreType.DMA((NRING,)), pltpu.SemaphoreType.DMA((4 * NMSG,)),
+            pltpu.SemaphoreType.DMA((7,)), pltpu.SemaphoreType.DMA((NRING,)), pltpu.SemaphoreType.DMA((4 * NMSG,)),
             pltpu.SemaphoreType.DMA((4 * NMSG,)), pltpu.SemaphoreType.DMA((7,)), pltpu.SemaphoreType.DMA((7,)),
         ],
         compiler_params=pltpu.CompilerParams(collective_id=0, has_side_effects=True, vmem_limit_bytes=54 * 2**20),

time: 86.2 us -> 85.5 us (level)
    pallas_call x1, Pallas kernels: 22.8 us -> 21.8 us  [attn_call(): pl.pallas_call(attn_kernel, out_shape=(cache, cache, pltpu.VMEM((2, 4, BA...]
where the time goes in v4:
time: 85.5 us; the launch traced here: 85.4 us
  Pallas kernels  84.6 us (99%)
    pallas_call x1, Pallas kernels, tail_call(): pl.pallas_call(tail_kernel, out_shape=(pltpu.VMEM((BATCH, D), bf16), pltp...  61.7 us
    pallas_call x1, Pallas kernels, attn_call(): pl.pallas_call(attn_kernel, out_shape=(cache, cache, pltpu.VMEM((2, 4, BA...  21.8 us

profile of v4, /device:TPU:0, one launch (start us, length us, event | category | flops | bytes accessed | tf_op | source)
XLA Modules:
  0.0 85.4 jit_solution(17765411138605700130)
XLA Ops:
  0.6 21.8 %attn.1 = (bf16[16384,512]{1,0:T(8,128)(2,1)}, bf16[16384,512]{1,0:T(8,128)(2,1)}, bf16[2,4,256,256]{3,2,1,0:T(8,128)(2,1)S(1)}) custom-call(s32[256]{0:T(256)} %len1_hbm.1, bf16[256,2048]{1,0:T(8,128)(2,1)} %x_hbm.3, s32[1,256]{1,0:T(1,128)} %bitcast.32, bf16[16384,512]{1,0:T(8,128)(2,1)} %bitcast.28, bf16[16384,512]{1,0:T(8,128)(2,1)} %bitcast.29, ...), custom_call_target="tpu_custom_call" | custom-call | flops 10000000000 | bytes 73400320 | tf_op jit(solution)/shard_map/attn/pallas_call | solution.py:235
  22.5 61.7 %tail.1 = (bf16[256,2048]{1,0:T(8,128)(2,1)S(1)}, f32[8,8,256]{2,1,0:T(8,128)S(1)}) custom-call(bf16[2,4,256,256]{3,2,1,0:T(8,128)(2,1)S(1)} %get-tuple-element.13.part_ref, bf16[256,2048]{1,0:T(8,128)(2,1)} %x_hbm.3, s32[1,256]{1,0:T(1,128)} %bitcast.36, bf16[16,128]{1,0:T(8,128)(2,1)} %bitcast.34, bf16[16,128]{1,0:T(8,128)(2,1)} %bitcast.35, ...), custom_call_target="tpu_custom_call" | custom-call | flops 20000000000 | bytes 83886080 | tf_op jit(solution)/shard_map/tail/pallas_call | solution.py:533
  84.2 1.0 %end.1 = (bf16[256,2048]{1,0:T(8,128)(2,1)}, f32[1,256]{1,0:T(1,128)}, f32[1,256]{1,0:T(1,128)}) custom-call(bf16[256,2048]{1,0:T(8,128)(2,1)S(1)} %get-tuple-element.14.y_ref, f32[8,8,256]{2,1,0:T(8,128)S(1)} %get-tuple-element.15.allst), custom_call_target="tpu_custom_call" | custom-call | tf_op jit(solution)/shard_map/end/pallas_call | solution.py:579
